TPU v7x, 128 devices: a whole 4x4x4 slice. The times are simulated.
128 devices in a mesh: batch: 1, ysp: 64 (over z, y, x), xsp: 2 (over core).
Axes of the slice: x: 4, y: 4, z: 4, core: 2. Of those that a mesh axis runs over, the one named last changes fastest.
Arguments:
- volume: bfloat16 [64, 64, 2048, 32], P('batch', 'xsp', 'ysp')
- filter_taps: float32 [3, 3, 21], replicated
- mix_weights: bfloat16 [3, 64, 64], replicated
- mix_bias: float32 [3, 64], replicated
Outputs:
- output: bfloat16 [64, 64, 2048, 32], P('batch', 'xsp', 'ysp')
All inputs are finite; a program needn't handle non-finite values.
Results may differ from a plain program's by a relative error of at most 0.00578.
Values are sent between devices in bfloat16 or wider.
A program may use at most 1 GiB of HBM per device.

v0:
```python
import jax
import jax.numpy as jnp
from jax import lax
from jax.sharding import PartitionSpec as P

PARTS_AXIS = "batch"
COL_AXIS = "ysp"
ROW_AXIS = "xsp"
DEPTH_TILE = 128


def band_matrix(tap_row, n_rows, n_cols, offset):
    tap_count = tap_row.shape[0]
    tap_index = jnp.arange(n_rows)[:, None] - jnp.arange(n_cols)[None, :] + offset
    tap_vals = tap_row.astype(jnp.bfloat16)[jnp.clip(tap_index, 0, tap_count - 1)]
    in_band = (tap_index >= 0) & (tap_index < tap_count)
    return jnp.where(in_band, tap_vals, jnp.zeros_like(tap_vals))


def depth_pass(operand, tap_row):
    half_width = (tap_row.shape[0] - 1) // 2
    depth_len = operand.shape[3]
    tile_len = min(DEPTH_TILE, depth_len)
    n_tiles = depth_len // tile_len
    tiled_op = operand.reshape(operand.shape[:3] + (n_tiles, tile_len))
    same_band = band_matrix(tap_row, tile_len, tile_len, half_width)
    if n_tiles == 1:
        filtered = jnp.einsum("cxyqa,ai->cxyqi", tiled_op, same_band, preferred_element_type=jnp.float32)
    else:
        band_cat = jnp.concatenate([same_band, band_matrix(tap_row, tile_len, tile_len, half_width - tile_len), band_matrix(tap_row, tile_len, tile_len, half_width + tile_len)], axis=1)
        spread = jnp.einsum("cxyqa,ai->cxyqi", tiled_op, band_cat, preferred_element_type=jnp.float32)
        own_tile = spread[..., :tile_len]
        to_next = spread[..., tile_len:2 * tile_len]
        to_prev = spread[..., 2 * tile_len:]
        zero_tile = jnp.zeros_like(own_tile[:, :, :, :1])
        filtered = own_tile + jnp.concatenate([zero_tile, to_next[:, :, :, :-1]], axis=3) + jnp.concatenate([to_prev[:, :, :, 1:], zero_tile], axis=3)
    return filtered.reshape(operand.shape).astype(jnp.bfloat16)


def halo_pass(operand, tap_row, dim_index, axis_name, axis_size, eq_form):
    half_width = (tap_row.shape[0] - 1) // 2
    extent = operand.shape[dim_index]
    tail_planes = lax.slice_in_dim(operand, extent - half_width, extent, axis=dim_index)
    head_planes = lax.slice_in_dim(operand, 0, half_width, axis=dim_index)
    if axis_size > 1:
        from_left = lax.ppermute(tail_planes, axis_name, [(source, source + 1) for source in range(axis_size - 1)])
        from_right = lax.ppermute(head_planes, axis_name, [(source + 1, source) for source in range(axis_size - 1)])
    else:
        from_left = jnp.zeros_like(tail_planes)
        from_right = jnp.zeros_like(head_planes)
    padded = jnp.concatenate([from_left, operand, from_right], axis=dim_index)
    toeplitz = band_matrix(tap_row, extent + 2 * half_width, extent, 0)
    return jnp.einsum(eq_form, padded, toeplitz, preferred_element_type=jnp.float32).astype(jnp.bfloat16)


def mix_residual(current, filtered, mix_mat, bias_vec):
    pre_act = jnp.einsum("cd,cxyz->dxyz", mix_mat, filtered, preferred_element_type=jnp.float32) + bias_vec[:, None, None, None]
    return (current.astype(jnp.float32) + jax.nn.gelu(pre_act, approximate=True)).astype(jnp.bfloat16)


def solution(mesh):
    x_count = mesh.shape[ROW_AXIS]
    y_count = mesh.shape[COL_AXIS]
    vol_spec = P(PARTS_AXIS, ROW_AXIS, COL_AXIS, None)

    def local_layers(volume, filter_taps, mix_weights, mix_bias):
        current = volume
        for layer_idx in range(filter_taps.shape[0]):
            x_filtered = halo_pass(current, filter_taps[layer_idx, 0], 1, ROW_AXIS, x_count, "cayz,ai->ciyz")
            xy_filtered = halo_pass(x_filtered, filter_taps[layer_idx, 1], 2, COL_AXIS, y_count, "cxaz,ai->cxiz")
            xyz_filtered = depth_pass(xy_filtered, filter_taps[layer_idx, 2])
            current = mix_residual(current, xyz_filtered, mix_weights[layer_idx], mix_bias[layer_idx])
        return current

    return jax.shard_map(local_layers, mesh=mesh, in_specs=(vol_spec, P(), P(), P()), out_specs=vol_spec, check_vma=False)
```

profile of v0, /device:TPU:96, one launch (start us, length us, event | category | flops | bytes accessed | tf_op | source)
XLA Modules:
  0.0 567.2 jit_solution(17776602651143374620)
XLA Ops:
  9.5 16.5 %copy.36 = bf16[64,32,32,32]{0,1,3,2:T(8,128)(2,1)} copy(bf16[64,32,32,32]{0,3,2,1:T(8,128)(2,1)} %param.4) | data formatting | bytes 8388608 | tf_op args[0]
  26.1 10.0 %gather_fusion.1 = bf16[1664]{0:T(1024)(128)(2,1)S(1)} fusion(bf16[21]{0:T(256)(128)(2,1)S(1)} %get-tuple-element.24, s32[2048]{0:T(1024)S(1)} %pad_clamp_fusion), kind=kCustom, calls=%fused_computation.1 | custom fusion | bytes 13312 | tf_op jit(solution)/shard_map/gather | solution.py:15
  36.2 6.7 %copy.35 = bf16[64,10,32,32]{0,1,3,2:T(8,128)(2,1)} copy(bf16[64,10,32,32]{0,3,2,1:T(8,128)(2,1)} %collective-permute-done) | data formatting | bytes 2621440 | tf_op jit(solution)/shard_map/ppermute | solution.py:46
  42.9 6.7 %copy.37 = bf16[64,10,32,32]{0,1,3,2:T(8,128)(2,1)} copy(bf16[64,10,32,32]{0,3,2,1:T(8,128)(2,1)} %collective-permute-done.1) | data formatting | bytes 2621440 | tf_op jit(solution)/shard_map/ppermute | solution.py:47
  49.6 15.5 %convert_bitcast_fusion.5 = bf16[64,32,32,32]{0,1,3,2:T(8,128)(2,1)} fusion(bf16[64,10,32,32]{0,1,3,2:T(8,128)(2,1)} %copy.37, bf16[64,32,32,32]{0,1,3,2:T(8,128)(2,1)} %copy.36, bf16[64,10,32,32]{0,1,3,2:T(8,128)(2,1)} %copy.35, bf16[52,32]{1,0:T(8,128)(2,1)S(1)} %reshape.101), kind=kOutput, calls=%fused_computation.74 | convolution fusion | flops 240656512 | bytes 11013376 | tf_op jit(solution)/shard_map/cayz,ai->ciyz/dot_general | solution.py:53
  73.6 6.7 %collective-permute-start.3 = (bf16[64,32,10,32]{0,1,3,2:T(8,128)(2,1)S(1)}, bf16[64,32,10,32]{0,1,3,2:T(8,128)(2,1)}, u32[]{:S(2)}, u32[]{:S(2)}) collective-permute-start(bf16[64,32,10,32]{0,1,3,2:T(8,128)(2,1)S(1)} %get-tuple-element.14), channel_id=1, source_target_pairs={{2,0},{4,2},{6,4},{8,6},{10,8},{12,10},{14,12},{16,14},{18,16},{20... | collective-permute-start | bytes 3932168 | tf_op jit(solution)/shard_map/ppermute | solution.py:47
  80.2 9.7 %gather_fusion = bf16[1664]{0:T(1024)(128)(2,1)S(1)} fusion(bf16[21]{0:T(256)(128)(2,1)S(1)} %get-tuple-element.25, s32[2048]{0:T(1024)S(1)} %pad_clamp_fusion), kind=kCustom, calls=%fused_computation | custom fusion | bytes 13312 | tf_op jit(solution)/shard_map/gather | solution.py:15
  90.2 6.5 %gather_fusion.2 = bf16[1024]{0:T(1024)(128)(2,1)S(1)} fusion(bf16[21]{0:T(256)(128)(2,1)S(1)} %get-tuple-element.23, s32[1024]{0:T(1024)S(1)} %broadcast_clamp_fusion), kind=kCustom, calls=%fused_computation.2 | custom fusion | bytes 8192 | tf_op jit(solution)/shard_map/gather | solution.py:15
  96.8 37.5 %collective-permute-done.2 = bf16[64,32,10,32]{0,1,3,2:T(8,128)(2,1)} collective-permute-done((bf16[64,32,10,32]{0,1,3,2:T(8,128)(2,1)}, bf16[64,32,10,32]{0,1,3,2:T(8,128)(2,1)}, u32[]{:S(2)}, u32[]{:S(2)}) %collective-permute-start.2) | collective-permute-done | bytes 1310752 | tf_op jit(solution)/shard_map/ppermute | solution.py:46
  136.0 21.1 %pad_maximum_fusion = bf16[64,32,52,32]{0,1,3,2:T(8,128)(2,1)} fusion(bf16[64,32,10,32]{0,1,3,2:T(8,128)(2,1)} %collective-permute-done.3, bf16[64,32,32,32]{0,1,3,2:T(8,128)(2,1)} %convert_bitcast_fusion.5, bf16[64,32,10,32]{0,1,3,2:T(8,128)(2,1)} %collective-permute-done.2), kind=kLoop, calls=%fused_computation.55 | loop fusion | flops 6815744 | bytes 13631488 | tf_op jit(solution)/shard_map/concatenate | solution.py:51
  157.1 27.7 %convert_bitcast_fusion.4 = bf16[64,32,32,32]{0,2,3,1:T(8,128)(2,1)} fusion(bf16[64,32,52,32]{0,1,3,2:T(8,128)(2,1)} %pad_maximum_fusion, bf16[52,32]{1,0:T(8,128)(2,1)S(1)} %reshape.93), kind=kOutput, calls=%fused_computation.73 | convolution fusion | flops 220209280 | bytes 11013376 | tf_op jit(solution)/shard_map/cxaz,ai->cxiz/dot_general | solution.py:53
  184.8 16.8 %fusion.8 = bf16[64,32,32,32]{0,3,2,1:T(8,128)(2,1)} fusion(bf16[64,32,32,32]{0,3,2,1:T(8,128)(2,1)} %param.4, f32[64]{0:T(128)S(1)} %get-tuple-element.27, bf16[64,32,32,32]{0,2,3,1:T(8,128)(2,1)} %convert_bitcast_fusion.4, bf16[3,64,64]{2,1,0:T(8,128)(2,1)S(1)} %copy-done.2, bf16[32,32]{1,0:T(8,128)(2,1)S(1)} %reshape.109), kind=kOutput, calls=%fused_computation.20 | convolution fusion | flops 429922304 | bytes 12608000 | tf_op jit(solution)/shard_map/cd,cxyz->dxyz/dot_general | solution.py:57
  213.4 10.2 %gather_fusion.4 = bf16[1664]{0:T(1024)(128)(2,1)S(1)} fusion(bf16[21]{0:T(256)(128)(2,1)S(1)} %get-tuple-element.21, s32[2048]{0:T(1024)S(1)} %pad_clamp_fusion), kind=kCustom, calls=%fused_computation.4 | custom fusion | bytes 13312 | tf_op jit(solution)/shard_map/gather | solution.py:15
  223.6 12.6 %pad_maximum_fusion.1 = bf16[64,52,32,32]{0,3,2,1:T(8,128)(2,1)} fusion(bf16[64,10,32,32]{0,3,2,1:T(8,128)(2,1)} %collective-permute-done.5, bf16[64,32,32,32]{0,3,2,1:T(8,128)(2,1)} %fusion.8, bf16[64,10,32,32]{0,3,2,1:T(8,128)(2,1)} %collective-permute-done.4), kind=kLoop, calls=%fused_computation.56 | loop fusion | flops 6815744 | bytes 13631488 | tf_op jit(solution)/shard_map/concatenate | solution.py:51
  236.3 19.9 %convert_bitcast_fusion.3 = bf16[64,32,32,32]{0,1,3,2:T(8,128)(2,1)} fusion(bf16[64,52,32,32]{0,3,2,1:T(8,128)(2,1)} %pad_maximum_fusion.1, bf16[52,32]{1,0:T(8,128)(2,1)S(1)} %reshape.125), kind=kOutput, calls=%fused_computation.71 | convolution fusion | flops 220209280 | bytes 11013376 | tf_op jit(solution)/shard_map/cayz,ai->ciyz/dot_general | solution.py:53
  263.0 8.3 %collective-permute-start.7 = (bf16[64,32,10,32]{0,1,3,2:T(8,128)(2,1)S(1)}, bf16[64,32,10,32]{0,1,3,2:T(8,128)(2,1)}, u32[]{:S(2)}, u32[]{:S(2)}) collective-permute-start(bf16[64,32,10,32]{0,1,3,2:T(8,128)(2,1)S(1)} %get-tuple-element.10), channel_id=1, source_target_pairs={{2,0},{4,2},{6,4},{8,6},{10,8},{12,10},{14,12},{16,14},{18,16},{20... | collective-permute-start | bytes 3932168 | tf_op jit(solution)/shard_map/ppermute | solution.py:47
  271.4 9.7 %gather_fusion.3 = bf16[1664]{0:T(1024)(128)(2,1)S(1)} fusion(bf16[21]{0:T(256)(128)(2,1)S(1)} %get-tuple-element.22, s32[2048]{0:T(1024)S(1)} %pad_clamp_fusion), kind=kCustom, calls=%fused_computation.3 | custom fusion | bytes 13312 | tf_op jit(solution)/shard_map/gather | solution.py:15
  281.2 6.5 %gather_fusion.5 = bf16[1024]{0:T(1024)(128)(2,1)S(1)} fusion(bf16[21]{0:T(256)(128)(2,1)S(1)} %get-tuple-element.20, s32[1024]{0:T(1024)S(1)} %broadcast_clamp_fusion), kind=kCustom, calls=%fused_computation.5 | custom fusion | bytes 8192 | tf_op jit(solution)/shard_map/gather | solution.py:15
  287.8 37.5 %collective-permute-done.6 = bf16[64,32,10,32]{0,1,3,2:T(8,128)(2,1)} collective-permute-done((bf16[64,32,10,32]{0,1,3,2:T(8,128)(2,1)}, bf16[64,32,10,32]{0,1,3,2:T(8,128)(2,1)}, u32[]{:S(2)}, u32[]{:S(2)}) %collective-permute-start.6) | collective-permute-done | bytes 1310752 | tf_op jit(solution)/shard_map/ppermute | solution.py:46
  327.0 12.8 %pad_maximum_fusion.2 = bf16[64,32,52,32]{0,1,3,2:T(8,128)(2,1)} fusion(bf16[64,32,10,32]{0,1,3,2:T(8,128)(2,1)} %collective-permute-done.7, bf16[64,32,32,32]{0,1,3,2:T(8,128)(2,1)} %convert_bitcast_fusion.3, bf16[64,32,10,32]{0,1,3,2:T(8,128)(2,1)} %collective-permute-done.6), kind=kLoop, calls=%fused_computation.57 | loop fusion | flops 6815744 | bytes 13631488 | tf_op jit(solution)/shard_map/concatenate | solution.py:51
  339.8 27.7 %convert_bitcast_fusion.2 = bf16[64,32,32,32]{0,2,3,1:T(8,128)(2,1)} fusion(bf16[64,32,52,32]{0,1,3,2:T(8,128)(2,1)} %pad_maximum_fusion.2, bf16[52,32]{1,0:T(8,128)(2,1)S(1)} %reshape.117), kind=kOutput, calls=%fused_computation.70 | convolution fusion | flops 220209280 | bytes 11013376 | tf_op jit(solution)/shard_map/cxaz,ai->cxiz/dot_general | solution.py:53
  367.4 16.8 %fusion.17 = bf16[64,32,32,32]{0,3,2,1:T(8,128)(2,1)} fusion(bf16[64,32,32,32]{0,3,2,1:T(8,128)(2,1)} %fusion.8, f32[64]{0:T(128)S(1)} %get-tuple-element.28, bf16[64,32,32,32]{0,2,3,1:T(8,128)(2,1)} %convert_bitcast_fusion.2, bf16[3,64,64]{2,1,0:T(8,128)(2,1)S(1)} %copy-done.2, bf16[32,32]{1,0:T(8,128)(2,1)S(1)} %reshape.133), kind=kOutput, calls=%fused_computation.29 | convolution fusion | flops 429922304 | bytes 12608000 | tf_op jit(solution)/shard_map/cd,cxyz->dxyz/dot_general | solution.py:57
  396.1 10.2 %gather_fusion.7 = bf16[1664]{0:T(1024)(128)(2,1)S(1)} fusion(bf16[21]{0:T(256)(128)(2,1)S(1)} %get-tuple-element.18, s32[2048]{0:T(1024)S(1)} %pad_clamp_fusion), kind=kCustom, calls=%fused_computation.7 | custom fusion | bytes 13312 | tf_op jit(solution)/shard_map/gather | solution.py:15
  406.4 12.6 %pad_maximum_fusion.3 = bf16[64,52,32,32]{0,3,2,1:T(8,128)(2,1)} fusion(bf16[64,10,32,32]{0,3,2,1:T(8,128)(2,1)} %collective-permute-done.9, bf16[64,32,32,32]{0,3,2,1:T(8,128)(2,1)} %fusion.17, bf16[64,10,32,32]{0,3,2,1:T(8,128)(2,1)} %collective-permute-done.8), kind=kLoop, calls=%fused_computation.58 | loop fusion | flops 6815744 | bytes 13631488 | tf_op jit(solution)/shard_map/concatenate | solution.py:51
  419.0 19.9 %convert_bitcast_fusion.1 = bf16[64,32,32,32]{0,1,3,2:T(8,128)(2,1)} fusion(bf16[64,52,32,32]{0,3,2,1:T(8,128)(2,1)} %pad_maximum_fusion.3, bf16[52,32]{1,0:T(8,128)(2,1)S(1)} %reshape.149), kind=kOutput, calls=%fused_computation.68 | convolution fusion | flops 220209280 | bytes 11013376 | tf_op jit(solution)/shard_map/cayz,ai->ciyz/dot_general | solution.py:53
  445.8 8.3 %collective-permute-start.11 = (bf16[64,32,10,32]{0,1,3,2:T(8,128)(2,1)S(1)}, bf16[64,32,10,32]{0,1,3,2:T(8,128)(2,1)}, u32[]{:S(2)}, u32[]{:S(2)}) collective-permute-start(bf16[64,32,10,32]{0,1,3,2:T(8,128)(2,1)S(1)} %get-tuple-element.6), channel_id=1, source_target_pairs={{2,0},{4,2},{6,4},{8,6},{10,8},{12,10},{14,12},{16,14},{18,16},{20... | collective-permute-start | bytes 3932168 | tf_op jit(solution)/shard_map/ppermute | solution.py:47
  454.2 9.7 %gather_fusion.6 = bf16[1664]{0:T(1024)(128)(2,1)S(1)} fusion(bf16[21]{0:T(256)(128)(2,1)S(1)} %get-tuple-element.19, s32[2048]{0:T(1024)S(1)} %pad_clamp_fusion), kind=kCustom, calls=%fused_computation.6 | custom fusion | bytes 13312 | tf_op jit(solution)/shard_map/gather | solution.py:15
  464.0 6.5 %gather_fusion.8 = bf16[1024]{0:T(1024)(128)(2,1)S(1)} fusion(bf16[21]{0:T(256)(128)(2,1)S(1)} %get-tuple-element.17, s32[1024]{0:T(1024)S(1)} %broadcast_clamp_fusion), kind=kCustom, calls=%fused_computation.8 | custom fusion | bytes 8192 | tf_op jit(solution)/shard_map/gather | solution.py:15
  470.6 37.5 %collective-permute-done.10 = bf16[64,32,10,32]{0,1,3,2:T(8,128)(2,1)} collective-permute-done((bf16[64,32,10,32]{0,1,3,2:T(8,128)(2,1)}, bf16[64,32,10,32]{0,1,3,2:T(8,128)(2,1)}, u32[]{:S(2)}, u32[]{:S(2)}) %collective-permute-start.10) | collective-permute-done | bytes 1310752 | tf_op jit(solution)/shard_map/ppermute | solution.py:46
  509.8 12.8 %pad_maximum_fusion.4 = bf16[64,32,52,32]{0,1,3,2:T(8,128)(2,1)} fusion(bf16[64,32,10,32]{0,1,3,2:T(8,128)(2,1)} %collective-permute-done.11, bf16[64,32,32,32]{0,1,3,2:T(8,128)(2,1)} %convert_bitcast_fusion.1, bf16[64,32,10,32]{0,1,3,2:T(8,128)(2,1)} %collective-permute-done.10), kind=kLoop, calls=%fused_computation.59 | loop fusion | flops 6815744 | bytes 13631488 | tf_op jit(solution)/shard_map/concatenate | solution.py:51
  522.5 27.6 %convert_bitcast_fusion = bf16[64,32,32,32]{0,2,3,1:T(8,128)(2,1)} fusion(bf16[64,32,52,32]{0,1,3,2:T(8,128)(2,1)} %pad_maximum_fusion.4, bf16[52,32]{1,0:T(8,128)(2,1)S(1)} %reshape.141), kind=kOutput, calls=%fused_computation.67 | convolution fusion | flops 220209280 | bytes 11013376 | tf_op jit(solution)/shard_map/cxaz,ai->cxiz/dot_general | solution.py:53
  550.2 16.8 %fusion.26 = bf16[64,32,32,32]{0,3,2,1:T(8,128)(2,1)} fusion(bf16[64,32,32,32]{0,3,2,1:T(8,128)(2,1)} %fusion.17, f32[64]{0:T(128)S(1)} %get-tuple-element.26, bf16[64,32,32,32]{0,2,3,1:T(8,128)(2,1)} %convert_bitcast_fusion, bf16[3,64,64]{2,1,0:T(8,128)(2,1)S(1)} %copy-done.2, bf16[32,32]{1,0:T(8,128)(2,1)S(1)} %reshape.157), kind=kOutput, calls=%fused_computation.38 | convolution fusion | flops 429922304 | bytes 12608000 | tf_op jit(solution)/shard_map/cd,cxyz->dxyz/dot_general | solution.py:57
  (48 shorter events, 61.3 us)
Async XLA Ops:
  0.0 26.0 %copy-start = (f32[3,3,21]{2,1,0:T(4,128)S(1)}, f32[3,3,21]{2,1,0:T(4,128)}, u32[]{:S(2)}) copy-start(f32[3,3,21]{2,1,0:T(4,128)} %param.5) | copy-start | bytes 2272
  4.9 31.2 %collective-permute-start = (bf16[64,10,32,32]{0,3,2,1:T(8,128)(2,1)}, bf16[64,10,32,32]{0,3,2,1:T(8,128)(2,1)}, u32[]{:S(2)}, u32[]{:S(2)}) collective-permute-start(bf16[64,10,32,32]{0,3,2,1:T(8,128)(2,1)} %get-tuple-element.15), channel_id=1, source_target_pairs={{0,1},{2,3},{4,5},{6,7},{8,9},{10,11},{12,13},{14,15},{16,17},{18,... | collective-permute-start | bytes 3932168 | tf_op jit(solution)/shard_map/ppermute | solution.py:46
  8.2 34.7 %collective-permute-start.1 = (bf16[64,10,32,32]{0,3,2,1:T(8,128)(2,1)S(1)}, bf16[64,10,32,32]{0,3,2,1:T(8,128)(2,1)}, u32[]{:S(2)}, u32[]{:S(2)}) collective-permute-start(bf16[64,10,32,32]{0,3,2,1:T(8,128)(2,1)S(1)} %get-tuple-element.16), channel_id=1, source_target_pairs={{1,0},{3,2},{5,4},{7,6},{9,8},{11,10},{13,12},{15,14},{17,16},{19,... | collective-permute-start | bytes 3932168 | tf_op jit(solution)/shard_map/ppermute | solution.py:47
  70.0 26.7 %copy-start.1 = (f32[3,64]{1,0:T(4,128)S(1)}, f32[3,64]{1,0:T(4,128)}, u32[]{:S(2)}) copy-start(f32[3,64]{1,0:T(4,128)} %param.7) | copy-start | bytes 2308
  70.0 64.2 %collective-permute-start.2 = (bf16[64,32,10,32]{0,1,3,2:T(8,128)(2,1)}, bf16[64,32,10,32]{0,1,3,2:T(8,128)(2,1)}, u32[]{:S(2)}, u32[]{:S(2)}) collective-permute-start(bf16[64,32,10,32]{0,1,3,2:T(8,128)(2,1)} %get-tuple-element.13), channel_id=1, source_target_pairs={{0,2},{2,4},{4,6},{6,8},{8,10},{10,12},{12,14},{14,16},{16,18},{18... | collective-permute-start | bytes 3932168 | tf_op jit(solution)/shard_map/ppermute | solution.py:46
  73.6 62.4 %collective-permute-start.3 = (bf16[64,32,10,32]{0,1,3,2:T(8,128)(2,1)S(1)}, bf16[64,32,10,32]{0,1,3,2:T(8,128)(2,1)}, u32[]{:S(2)}, u32[]{:S(2)}) collective-permute-start(bf16[64,32,10,32]{0,1,3,2:T(8,128)(2,1)S(1)} %get-tuple-element.14), channel_id=1, source_target_pairs={{2,0},{4,2},{6,4},{8,6},{10,8},{12,10},{14,12},{16,14},{18,16},{20... | collective-permute-start | bytes 3932168 | tf_op jit(solution)/shard_map/ppermute | solution.py:47
  157.1 27.7 %copy-start.2 = (bf16[3,64,64]{2,1,0:T(8,128)(2,1)S(1)}, bf16[3,64,64]{2,1,0:T(8,128)(2,1)}, u32[]{:S(2)}) copy-start(bf16[3,64,64]{2,1,0:T(8,128)(2,1)} %param.6) | copy-start | bytes 73732
  206.6 17.0 %collective-permute-start.4 = (bf16[64,10,32,32]{0,3,2,1:T(8,128)(2,1)}, bf16[64,10,32,32]{0,3,2,1:T(8,128)(2,1)}, u32[]{:S(2)}, u32[]{:S(2)}) collective-permute-start(bf16[64,10,32,32]{0,3,2,1:T(8,128)(2,1)} %get-tuple-element.11), channel_id=1, source_target_pairs={{0,1},{2,3},{4,5},{6,7},{8,9},{10,11},{12,13},{14,15},{16,17},{18,... | collective-permute-start | bytes 3932168 | tf_op jit(solution)/shard_map/ppermute | solution.py:46
  212.1 11.5 %collective-permute-start.5 = (bf16[64,10,32,32]{0,3,2,1:T(8,128)(2,1)S(1)}, bf16[64,10,32,32]{0,3,2,1:T(8,128)(2,1)}, u32[]{:S(2)}, u32[]{:S(2)}) collective-permute-start(bf16[64,10,32,32]{0,3,2,1:T(8,128)(2,1)S(1)} %get-tuple-element.12), channel_id=1, source_target_pairs={{1,0},{3,2},{5,4},{7,6},{9,8},{11,10},{13,12},{15,14},{17,16},{19,... | collective-permute-start | bytes 3932168 | tf_op jit(solution)/shard_map/ppermute | solution.py:47
  261.1 64.1 %collective-permute-start.6 = (bf16[64,32,10,32]{0,1,3,2:T(8,128)(2,1)}, bf16[64,32,10,32]{0,1,3,2:T(8,128)(2,1)}, u32[]{:S(2)}, u32[]{:S(2)}) collective-permute-start(bf16[64,32,10,32]{0,1,3,2:T(8,128)(2,1)} %get-tuple-element.9), channel_id=1, source_target_pairs={{0,2},{2,4},{4,6},{6,8},{8,10},{10,12},{12,14},{14,16},{16,18},{18... | collective-permute-start | bytes 3932168 | tf_op jit(solution)/shard_map/ppermute | solution.py:46
  263.0 63.9 %collective-permute-start.7 = (bf16[64,32,10,32]{0,1,3,2:T(8,128)(2,1)S(1)}, bf16[64,32,10,32]{0,1,3,2:T(8,128)(2,1)}, u32[]{:S(2)}, u32[]{:S(2)}) collective-permute-start(bf16[64,32,10,32]{0,1,3,2:T(8,128)(2,1)S(1)} %get-tuple-element.10), channel_id=1, source_target_pairs={{2,0},{4,2},{6,4},{8,6},{10,8},{12,10},{14,12},{16,14},{18,16},{20... | collective-permute-start | bytes 3932168 | tf_op jit(solution)/shard_map/ppermute | solution.py:47
  389.2 17.2 %collective-permute-start.8 = (bf16[64,10,32,32]{0,3,2,1:T(8,128)(2,1)}, bf16[64,10,32,32]{0,3,2,1:T(8,128)(2,1)}, u32[]{:S(2)}, u32[]{:S(2)}) collective-permute-start(bf16[64,10,32,32]{0,3,2,1:T(8,128)(2,1)} %get-tuple-element.7), channel_id=1, source_target_pairs={{0,1},{2,3},{4,5},{6,7},{8,9},{10,11},{12,13},{14,15},{16,17},{18,... | collective-permute-start | bytes 3932168 | tf_op jit(solution)/shard_map/ppermute | solution.py:46
  394.9 11.5 %collective-permute-start.9 = (bf16[64,10,32,32]{0,3,2,1:T(8,128)(2,1)S(1)}, bf16[64,10,32,32]{0,3,2,1:T(8,128)(2,1)}, u32[]{:S(2)}, u32[]{:S(2)}) collective-permute-start(bf16[64,10,32,32]{0,3,2,1:T(8,128)(2,1)S(1)} %get-tuple-element.8), channel_id=1, source_target_pairs={{1,0},{3,2},{5,4},{7,6},{9,8},{11,10},{13,12},{15,14},{17,16},{19,... | collective-permute-start | bytes 3932168 | tf_op jit(solution)/shard_map/ppermute | solution.py:47
  443.9 64.1 %collective-permute-start.10 = (bf16[64,32,10,32]{0,1,3,2:T(8,128)(2,1)}, bf16[64,32,10,32]{0,1,3,2:T(8,128)(2,1)}, u32[]{:S(2)}, u32[]{:S(2)}) collective-permute-start(bf16[64,32,10,32]{0,1,3,2:T(8,128)(2,1)} %get-tuple-element.5), channel_id=1, source_target_pairs={{0,2},{2,4},{4,6},{6,8},{8,10},{10,12},{12,14},{14,16},{16,18},{18... | collective-permute-start | bytes 3932168 | tf_op jit(solution)/shard_map/ppermute | solution.py:46
  445.8 63.9 %collective-permute-start.11 = (bf16[64,32,10,32]{0,1,3,2:T(8,128)(2,1)S(1)}, bf16[64,32,10,32]{0,1,3,2:T(8,128)(2,1)}, u32[]{:S(2)}, u32[]{:S(2)}) collective-permute-start(bf16[64,32,10,32]{0,1,3,2:T(8,128)(2,1)S(1)} %get-tuple-element.6), channel_id=1, source_target_pairs={{2,0},{4,2},{6,4},{8,6},{10,8},{12,10},{14,12},{16,14},{18,16},{20... | collective-permute-start | bytes 3932168 | tf_op jit(solution)/shard_map/ppermute | solution.py:47
where the time goes:
time: 577 us; the launch traced here: 567 us
  matrix products  189 us (33%)
  local copies, waits for them, and re-layouts  139 us (24%)
  waiting for transfers between devices  118 us (20%)
  other arithmetic  72 us (12%)
  starting transfers between devices  48.9 us (8%)
    dot_general x6, matrix products, halo_pass(): jnp.einsum(eq_form, padded, toeplitz, preferred_element_type=jnp.float32)  138 us
    ppermute x6, waiting for transfers between devices, halo_pass(): lax.ppermute(tail_planes, axis_name, [(source, source + 1) for source in...  112 us
    gather x18, local copies, waits for them, and re-layouts, band_matrix(): tap_row.astype(jnp.bfloat16)[jnp.clip(tap_index, 0, tap_count - 1)]  79.8 us
    concatenate x5, other arithmetic, halo_pass(): padded = jnp.concatenate([from_left, operand, from_right], axis=dim_index)  71.9 us
    dot_general x3, matrix products, mix_residual(): jnp.einsum('cd,cxyz->dxyz', mix_mat, filtered, preferred_element_type=jnp...  50.4 us
    slice x6, local copies, waits for them, and re-layouts, halo_pass(): lax.slice_in_dim(operand, extent - half_width, extent, axis=dim_index)  29.6 us
    ppermute x6, starting transfers between devices, halo_pass(): lax.ppermute(head_planes, axis_name, [(source + 1, source) for source in...  27.2 us
    ppermute x6, starting transfers between devices, halo_pass(): lax.ppermute(tail_planes, axis_name, [(source, source + 1) for source in...  21.8 us
  transfers between devices with their start and end apart: 12, of which 6 were waited for; matrix products, arithmetic and copies ran while one was open for 18% of the time, Pallas kernels for 0%

commit v1 on v0

v1 whole, which is shorter than its diff:
```python
import functools

import jax
import jax.numpy as jnp
from jax import lax
from jax.experimental import pallas as pl
from jax.experimental.pallas import tpu as pltpu
from jax.sharding import PartitionSpec as P

PARTS_AXIS = "batch"
COL_AXIS = "ysp"
ROW_AXIS = "xsp"
H = 10
TAPS = 2 * H + 1
LAYERS = 3
C = 64
BX = 32
BY = 32
BZ = 32
ZL = 16
LANES = 128
CH = 8
NCH = BX // CH
WIN = CH + 2 * H
XS = BX + H
YS = BY + 2 * H
F32 = jnp.float32
BF16 = jnp.bfloat16


def band_times_eye(tap, rows, cols, inner, shift):
    i = lax.broadcasted_iota(jnp.int32, (rows, cols), 0)
    j = lax.broadcasted_iota(jnp.int32, (rows, cols), 1)
    t = j // inner - i // inner + shift
    acc = jnp.zeros((rows, cols), F32)
    for n in range(TAPS):
        acc = jnp.where(t == n, tap(n), acc)
    return jnp.where(i % inner == j % inner, acc, 0.0).astype(BF16)


def kernel(y_count, vol, taps, wmat, bias, out, stage, vbuf, ubuf, tx, ty, tz, w4, in_sem, out_sem, ysend, yrecv, xsend, xrecv):
    xi = lax.axis_index(ROW_AXIS)
    yi = lax.axis_index(COL_AXIS)
    own = xi * H
    has_left = yi > 0
    has_right = yi < y_count - 1
    left = lax.rem(yi + y_count - 1, y_count)
    right = lax.rem(yi + 1, y_count)

    def x_of(k):
        return jnp.where(xi == 0, CH * k, BX - CH - CH * k)

    def load(k):
        x0 = x_of(k)
        return pltpu.make_async_copy(vol.at[pl.ds(x0, CH)], stage.at[k], in_sem.at[k])

    for k in range(NCH):
        load(k).start()

    barrier = pltpu.get_barrier_semaphore()
    pl.semaphore_signal(barrier, inc=1, device_id={COL_AXIS: left})
    pl.semaphore_signal(barrier, inc=1, device_id={COL_AXIS: right})
    pl.semaphore_signal(barrier, inc=1, device_id={ROW_AXIS: 1 - xi})

    def y_copy(l, k, side):
        xs = pl.ds(x_of(k), CH)
        src = ubuf.at[l, xs, pl.ds(H, H)] if side == 0 else ubuf.at[l, xs, pl.ds(BY, H)]
        dst = ubuf.at[l, xs, pl.ds(H + BY, H)] if side == 0 else ubuf.at[l, xs, pl.ds(0, H)]
        return pltpu.make_async_remote_copy(
            src_ref=src, dst_ref=dst, send_sem=ysend.at[l, k, side], recv_sem=yrecv.at[l, k, side],
            device_id={COL_AXIS: left if side == 0 else right})

    def x_copy(l):
        src = jnp.where(xi == 0, BX - H, H)
        dst = jnp.where(xi == 0, 0, BX)
        return pltpu.make_async_remote_copy(
            src_ref=vbuf.at[l, pl.ds(src, H)], dst_ref=vbuf.at[l, pl.ds(dst, H)],
            send_sem=xsend.at[l], recv_sem=xrecv.at[l], device_id={ROW_AXIS: 1 - xi})

    def x_pass(l, k):
        x0 = x_of(k)
        slot = own + x0
        w0 = jnp.clip(slot - H, 0, XS - WIN)
        tx[...] = band_times_eye(lambda n: taps[l * 3, n], CH * ZL, WIN * ZL, ZL, w0 - slot + H)

        def body(j, carry):
            y0 = j * 4
            cols = [vbuf[l, pl.ds(w0, WIN), y0 + i].reshape(WIN * ZL, LANES) for i in range(4)]
            r = jnp.dot(tx[...], jnp.concatenate(cols, axis=1), preferred_element_type=F32).astype(BF16)
            for i in range(4):
                ubuf[l, pl.ds(x0, CH), H + y0 + i] = r[:, LANES * i:LANES * (i + 1)].reshape(CH, ZL, LANES)
            return carry

        lax.fori_loop(0, BY // 4, body, 0)

        @pl.when(has_left)
        def _():
            y_copy(l, k, 0).start()

        @pl.when(has_right)
        def _():
            y_copy(l, k, 1).start()

    def layer_mats(l):
        ty[...] = band_times_eye(lambda n: taps[l * 3 + 1, n], CH * ZL, WIN * ZL, ZL, 0)
        i = lax.broadcasted_iota(jnp.int32, (8 * BZ, 8 * BZ), 0)
        j = lax.broadcasted_iota(jnp.int32, (8 * BZ, 8 * BZ), 1)
        t = j - i + H
        acc = jnp.zeros((8 * BZ, 8 * BZ), F32)
        for n in range(TAPS):
            acc = jnp.where(t == n, taps[l * 3 + 2, n], acc)
        tz[...] = jnp.where(i // BZ == j // BZ, acc, 0.0).astype(BF16)
        w = wmat[l].astype(F32)
        w = jnp.concatenate([w, w], axis=1)
        w = jnp.concatenate([w, w], axis=1)
        w = jnp.concatenate([w, w, w, w], axis=0)
        i = lax.broadcasted_iota(jnp.int32, (4 * C, 4 * C), 0) // C
        j = lax.broadcasted_iota(jnp.int32, (4 * C, 4 * C), 1) // C
        keep = (i // 2 == j % 2) & (i % 2 == j // 2)
        w4[...] = jnp.where(keep, w, 0.0).astype(BF16)

    def y_pass(l, k):
        @pl.when(has_left)
        def _():
            y_copy(l, k, 1).wait_recv()

        @pl.when(has_right)
        def _():
            y_copy(l, k, 0).wait_recv()

        x0 = x_of(k)
        b = bias[pl.ds(l, 1), :]
        b = jnp.concatenate([b, b], axis=1)
        b = jnp.concatenate([b, b], axis=1)
        nxt = jnp.minimum(l + 1, LAYERS - 1)

        def body(it, carry):
            xq = x0 + 4 * (it // 4)
            y0 = pl.multiple_of(8 * (it % 4), 8)
            cols = [ubuf[l, xq + i, pl.ds(y0, WIN)].reshape(WIN * ZL, LANES) for i in range(4)]
            r = jnp.dot(ty[...], jnp.concatenate(cols, axis=1), preferred_element_type=F32).astype(BF16)
            zs = []
            for i in range(4):
                u = r[:, LANES * i:LANES * (i + 1)].reshape(4, 2, ZL, LANES)
                ya, yb = u[:, 0], u[:, 1]
                lo = jnp.concatenate([ya[:, :, :C], yb[:, :, :C]], axis=2)
                hi = jnp.concatenate([ya[:, :, C:], yb[:, :, C:]], axis=2)
                zs.append(jnp.concatenate([lo, hi], axis=1).reshape(4 * BZ, LANES))
            dz = jnp.concatenate([jnp.concatenate([zs[0], zs[1]], axis=0), jnp.concatenate([zs[2], zs[3]], axis=0)], axis=1)
            s = jnp.dot(tz[...], dz, preferred_element_type=F32).astype(BF16)
            lhs = []
            for h in range(2):
                sh = s[:, LANES * h:LANES * (h + 1)].reshape(8, 2, ZL, LANES)
                lhs.append(jnp.concatenate([sh[:, 0], sh[:, 1]], axis=2).reshape(8 * ZL, 2 * LANES))
            m = jnp.dot(jnp.concatenate(lhs, axis=0), w4[...], preferred_element_type=F32) + b
            m = jax.nn.gelu(m, approximate=True)
            for i in range(4):
                mi = m[64 * i:64 * (i + 1)].reshape(4, 1, ZL, 2 * LANES)
                mi = jnp.concatenate([mi[..., :LANES], mi[..., LANES:]], axis=1).reshape(8, ZL, LANES)
                old = vbuf[l, own + xq + i, pl.ds(y0, 8)].astype(F32)
                vbuf[nxt, own + xq + i, pl.ds(y0, 8)] = (old + mi).astype(BF16)
            return carry

        lax.fori_loop(0, 8, body, 0)

    def zero_planes(l, carry):
        vbuf[l, pl.ds(own + x_of(NCH - 1), CH)] = jnp.zeros((CH, BY, ZL, LANES), BF16)
        return carry

    lax.fori_loop(1, LAYERS, zero_planes, 0)

    def zero_halo(y0):
        def body(n, carry):
            ubuf[n // BX, n % BX, pl.ds(y0, H)] = jnp.zeros((H, ZL, LANES), BF16)
            return carry

        lax.fori_loop(0, LAYERS * BX, body, 0)

    def pack(k, carry):
        load(k).wait()
        x0 = x_of(k)

        def body(p, c):
            s = stage[k, p]
            vbuf[0, own + x0 + p] = jnp.concatenate([s[:, :ZL], s[:, ZL:]], axis=2)
            return c

        lax.fori_loop(0, CH, body, 0)
        return carry

    lax.fori_loop(0, NCH, pack, 0)
    pl.semaphore_wait(barrier, 3)
    x_copy(0).start()
    x_pass(0, 0)

    @pl.when(jnp.logical_not(has_left))
    def _():
        zero_halo(0)

    @pl.when(jnp.logical_not(has_right))
    def _():
        zero_halo(H + BY)

    def layer(l, carry):
        def xs(k, c):
            @pl.when(k == 2)
            def _():
                x_copy(l).wait()

            x_pass(l, k)
            return c

        lax.fori_loop(1, NCH, xs, 0)
        layer_mats(l)

        def ys(k, c):
            @pl.when((k == NCH - 1) & (l < LAYERS - 1))
            def _():
                x_pass(l + 1, 0)

            y_pass(l, k)

            @pl.when(l == LAYERS - 1)
            def _():
                store(k).start()

            return c

        lax.fori_loop(0, NCH, ys, 0)

        @pl.when(l < LAYERS - 1)
        def _():
            x_copy(l + 1).start()

        return carry

    def store(k):
        x0 = x_of(k)
        return pltpu.make_async_copy(vbuf.at[LAYERS - 1, pl.ds(own + x0, CH)], out.at[pl.ds(x0, CH)], out_sem.at[k])

    lax.fori_loop(0, LAYERS, layer, 0)

    def finish(n, carry):
        l, k = n // NCH, n % NCH

        @pl.when(has_left)
        def _():
            y_copy(l, k, 0).wait_send()

        @pl.when(has_right)
        def _():
            y_copy(l, k, 1).wait_send()

        return carry

    lax.fori_loop(0, LAYERS * NCH, finish, 0)
    for k in range(NCH):
        store(k).wait()


def unpack_kernel(src, dst):
    s = src[...]
    dst[:, :, :ZL, :] = s[:, :, :, :C]
    dst[:, :, ZL:, :] = s[:, :, :, C:]


def solution(mesh):
    y_count = mesh.shape[COL_AXIS]
    vol_spec = P(PARTS_AXIS, ROW_AXIS, COL_AXIS, None)
    any_spec = pl.BlockSpec(memory_space=pl.ANY)
    vmem_spec = pl.BlockSpec(memory_space=pltpu.VMEM)

    def local_layers(volume, filter_taps, mix_weights, mix_bias):
        vol = jnp.transpose(volume, (1, 2, 3, 0))
        taps = filter_taps.reshape(LAYERS * 3, TAPS)
        packed = pl.pallas_call(
            functools.partial(kernel, y_count),
            out_shape=jax.ShapeDtypeStruct((BX, BY, ZL, LANES), BF16),
            in_specs=[any_spec, pl.BlockSpec(memory_space=pltpu.SMEM), vmem_spec, vmem_spec],
            out_specs=any_spec,
            scratch_shapes=[
                pltpu.VMEM((NCH, CH, BY, BZ, C), BF16),
                pltpu.VMEM((LAYERS, XS, BY, ZL, LANES), BF16),
                pltpu.VMEM((LAYERS, BX, YS, ZL, LANES), BF16),
                pltpu.VMEM((CH * ZL, WIN * ZL), BF16),
                pltpu.VMEM((CH * ZL, WIN * ZL), BF16),
                pltpu.VMEM((8 * BZ, 8 * BZ), BF16),
                pltpu.VMEM((4 * C, 4 * C), BF16),
                pltpu.SemaphoreType.DMA((NCH,)),
                pltpu.SemaphoreType.DMA((NCH,)),
                pltpu.SemaphoreType.DMA((LAYERS, NCH, 2)),
                pltpu.SemaphoreType.DMA((LAYERS, NCH, 2)),
                pltpu.SemaphoreType.DMA((LAYERS,)),
                pltpu.SemaphoreType.DMA((LAYERS,)),
            ],
            compiler_params=pltpu.CompilerParams(collective_id=0, has_side_effects=True, vmem_limit_bytes=60 * 2**20),
        )(vol, taps, mix_weights, mix_bias)
        result = pl.pallas_call(
            unpack_kernel,
            grid=(8,),
            out_shape=jax.ShapeDtypeStruct((BX, BY, BZ, C), BF16),
            in_specs=[pl.BlockSpec((BX // 8, BY, ZL, LANES), lambda i: (i, 0, 0, 0))],
            out_specs=pl.BlockSpec((BX // 8, BY, BZ, C), lambda i: (i, 0, 0, 0)),
        )(packed)
        return jnp.transpose(result, (3, 0, 1, 2))

    return jax.shard_map(local_layers, mesh=mesh, in_specs=(vol_spec, P(), P(), P()), out_specs=vol_spec, check_vma=False)
```

time: 577 us -> 126 us (0.22); the launches traced: 567 us -> 126 us
  matrix products: 189 us -> 0 us
  local copies, waits for them, and re-layouts: 139 us -> 1.3 us
  Pallas kernels: 0 us -> 124 us
  waiting for transfers between devices: 118 us -> 0 us
  other arithmetic: 72 us -> 0 us
  starting transfers between devices: 48.9 us -> 0 us
    dot_general x9 -> x0, matrix products: 189 us -> none  [the longest x6 138 us: halo_pass(): jnp.einsum(eq_form, padded, toeplitz, preferred_element_type=jnp.float32)]
    pallas_call x0 -> x2, Pallas kernels: none -> 124 us  [the longest x1 116 us: local_layers(): pl.pallas_call(functools.partial(kernel, y_count), out_shape=jax.ShapeDty...]
    ppermute x12 -> x0, waiting for transfers between devices: 118 us -> none  [the longest x6 112 us: halo_pass(): lax.ppermute(tail_planes, axis_name, [(source, source + 1) for source in...]
    gather x18 -> x0, local copies, waits for them, and re-layouts: 79.8 us -> none  [band_matrix(): tap_row.astype(jnp.bfloat16)[jnp.clip(tap_index, 0, tap_count - 1)]]
    concatenate x5 -> x0, other arithmetic: 71.9 us -> none  [halo_pass(): padded = jnp.concatenate([from_left, operand, from_right], axis=dim_index)]
    ppermute x12 -> x0, starting transfers between devices: 48.9 us -> none  [the longest x6 27.2 us: halo_pass(): lax.ppermute(head_planes, axis_name, [(source + 1, source) for source in...]
    slice x6 -> x0, local copies, waits for them, and re-layouts: 29.6 us -> none  [halo_pass(): lax.slice_in_dim(operand, extent - half_width, extent, axis=dim_index)]
    unnamed x7 -> x0, local copies, waits for them, and re-layouts: 16.5 us -> none
  transfers between devices with their start and end apart: 12 -> 0, of which waited for: 6 -> 0; matrix products, arithmetic and copies ran while one was open for 18% -> 0% of each run, Pallas kernels for 0% -> 0%
where the time goes in v1:
time: 126 us
  Pallas kernels  124 us (98%)
  local copies, waits for them, and re-layouts  1.3 us (1%)
    pallas_call x1, Pallas kernels, local_layers(): pl.pallas_call(functools.partial(kernel, y_count), out_shape=jax.ShapeDty...  116 us
    pallas_call x1, Pallas kernels, local_layers(): pl.pallas_call(unpack_kernel, grid=(8,), out_shape=jax.ShapeDtypeStruct((...  8.31 us

profile of v1, /device:TPU:96, one launch (start us, length us, event | category | flops | bytes accessed | tf_op | source)
XLA Modules:
  0.0 125.7 jit_solution(8118000375334857351)
XLA Ops:
  0.0 1.3 %reshape.3.taps = f32[9,21]{1,0:T(8,128)} reshape(f32[3,3,21]{2,1,0:T(4,128)} %param.5) | data formatting | bytes 1512 | tf_op jit(solution)/shard_map/reshape | solution.py:275
  1.3 116.1 %shard_map.46.src = bf16[32,32,16,128]{3,2,1,0:T(8,128)(2,1)} custom-call(bf16[32,32,32,64]{3,2,1,0:T(8,128)(2,1)} %bitcast.2, f32[9,21]{1,0:T(8,128)} %reshape.3.taps, bf16[3,64,64]{2,1,0:T(8,128)(2,1)} %wmat.1, f32[3,64]{1,0:T(4,128)} %bias.1), custom_call_target="tpu_custom_call" | custom-call | tf_op jit(solution)/shard_map/pallas_call | solution.py:276
  117.4 8.3 %shard_map.47 = bf16[32,32,32,64]{3,2,1,0:T(8,128)(2,1)} custom-call(bf16[32,32,16,128]{3,2,1,0:T(8,128)(2,1)} %shard_map.46.src), custom_call_target="tpu_custom_call" | custom-call | tf_op jit(solution)/shard_map/pallas_call | solution.py:298

commit v2 on v1

v2 whole, which is shorter than its diff:
```python
import functools

import jax
import jax.numpy as jnp
from jax import lax
from jax.experimental import pallas as pl
from jax.experimental.pallas import tpu as pltpu
from jax.sharding import PartitionSpec as P

PARTS_AXIS = "batch"
COL_AXIS = "ysp"
ROW_AXIS = "xsp"
H = 10
TAPS = 2 * H + 1
LAYERS = 3
C = 64
BX = 32
BY = 32
BZ = 32
ZL = 16
LANES = 128
CH = 8
NCH = BX // CH
QUAD = 4
NQ = BX // QUAD
WIN = CH + 2 * H
XS = BX + H
YS = BY + 2 * H
SEGS = ((0, H), (BY - H, H), (H, BY - 2 * H))
F32 = jnp.float32
BF16 = jnp.bfloat16


def band_times_eye(tap, rows, cols, inner, shift):
    i = lax.broadcasted_iota(jnp.int32, (rows, cols), 0)
    j = lax.broadcasted_iota(jnp.int32, (rows, cols), 1)
    t = j // inner - i // inner + shift
    acc = jnp.zeros((rows, cols), F32)
    for n in range(TAPS):
        acc = jnp.where(t == n, tap(n), acc)
    return jnp.where(i % inner == j % inner, acc, 0.0).astype(BF16)


def kernel(y_count, vol, taps, wmat, bias, out, stage, vbuf, ubuf, tx, ty, tz, w4, in_sem, out_sem, ysend, yrecv, xsend, xrecv):
    xi = lax.axis_index(ROW_AXIS)
    yi = lax.axis_index(COL_AXIS)
    own = xi * H
    has_left = yi > 0
    has_right = yi < y_count - 1
    left = lax.rem(yi + y_count - 1, y_count)
    right = lax.rem(yi + 1, y_count)

    def x_of(k):
        return jnp.where(xi == 0, CH * k, BX - CH - CH * k)

    def xq_of(q):
        return jnp.where(xi == 0, QUAD * q, BX - QUAD - QUAD * q)

    def load(k, seg):
        ys = pl.ds(*SEGS[seg])
        return pltpu.make_async_copy(vol.at[pl.ds(x_of(k), CH), ys], stage.at[k, :, ys], in_sem.at[k, seg])

    for seg in range(2):
        for k in range(NCH - 1):
            load(k, seg).start()
    load(NCH - 1, 0).start()
    load(NCH - 1, 1).start()
    for k in range(NCH):
        load(k, 2).start()

    barrier = pltpu.get_barrier_semaphore()
    pl.semaphore_signal(barrier, inc=1, device_id={COL_AXIS: left})
    pl.semaphore_signal(barrier, inc=1, device_id={COL_AXIS: right})
    pl.semaphore_signal(barrier, inc=1, device_id={ROW_AXIS: 1 - xi})

    def y_copy(l, q, side):
        xs = pl.ds(xq_of(q), QUAD)
        src = ubuf.at[l, xs, pl.ds(H, H)] if side == 0 else ubuf.at[l, xs, pl.ds(BY, H)]
        dst = ubuf.at[l, xs, pl.ds(H + BY, H)] if side == 0 else ubuf.at[l, xs, pl.ds(0, H)]
        return pltpu.make_async_remote_copy(
            src_ref=src, dst_ref=dst, send_sem=ysend.at[l, q, side], recv_sem=yrecv.at[l, q, side],
            device_id={COL_AXIS: left if side == 0 else right})

    def x_copy(l):
        src = jnp.where(xi == 0, BX - H, H)
        dst = jnp.where(xi == 0, 0, BX)
        return pltpu.make_async_remote_copy(
            src_ref=vbuf.at[l, pl.ds(src, H)], dst_ref=vbuf.at[l, pl.ds(dst, H)],
            send_sem=xsend.at[l], recv_sem=xrecv.at[l], device_id={ROW_AXIS: 1 - xi})

    def window(k):
        slot = own + x_of(k)
        return jnp.clip(slot - H, 0, XS - WIN), slot

    def x_mat(l, k):
        with jax.named_scope("xmat"):
            w0, slot = window(k)
            tx[...] = band_times_eye(lambda n: taps[l, 0, n], CH * ZL, WIN * ZL, ZL, w0 - slot + H)

    def x_seg(l, k, seg):
        with jax.named_scope("xseg"):
            w0, _ = window(k)
            x0 = x_of(k)
            first, count = SEGS[seg]
            cols = [vbuf[l, pl.ds(w0, WIN), first + i].reshape(WIN * ZL, LANES) for i in range(count)]
            r = jnp.dot(tx[...], jnp.concatenate(cols, axis=1), preferred_element_type=F32).astype(BF16)
            for i in range(count):
                ubuf[l, pl.ds(x0, CH), H + first + i] = r[:, LANES * i:LANES * (i + 1)].reshape(CH, ZL, LANES)

    def y_send(l, k, side):
        @pl.when(has_left if side == 0 else has_right)
        def _():
            for j in range(CH // QUAD):
                y_copy(l, k * (CH // QUAD) + j, side).start()

    def x_pass(l, k):
        x_mat(l, k)
        x_seg(l, k, 0)
        y_send(l, k, 0)
        x_seg(l, k, 1)
        y_send(l, k, 1)
        x_seg(l, k, 2)

    def layer_mats(l):
        ty[...] = band_times_eye(lambda n: taps[l, 1, n], CH * ZL, WIN * ZL, ZL, 0)
        i = lax.broadcasted_iota(jnp.int32, (8 * BZ, 8 * BZ), 0)
        j = lax.broadcasted_iota(jnp.int32, (8 * BZ, 8 * BZ), 1)
        t = j - i + H
        acc = jnp.zeros((8 * BZ, 8 * BZ), F32)
        for n in range(TAPS):
            acc = jnp.where(t == n, taps[l, 2, n], acc)
        tz[...] = jnp.where(i // BZ == j // BZ, acc, 0.0).astype(BF16)
        w = wmat[l].astype(F32)
        w = jnp.concatenate([w, w], axis=1)
        w = jnp.concatenate([w, w], axis=1)
        w = jnp.concatenate([w, w, w, w], axis=0)
        i = lax.broadcasted_iota(jnp.int32, (4 * C, 4 * C), 0) // C
        j = lax.broadcasted_iota(jnp.int32, (4 * C, 4 * C), 1) // C
        keep = (i // 2 == j % 2) & (i % 2 == j // 2)
        w4[...] = jnp.where(keep, w, 0.0).astype(BF16)

    def y_quad(l, q):
        with jax.named_scope("ywait"):
            @pl.when(has_left)
            def _():
                y_copy(l, q, 1).wait_recv()

            @pl.when(has_right)
            def _():
                y_copy(l, q, 0).wait_recv()

        with jax.named_scope("yquad"):
            xq = xq_of(q)
            b = bias[pl.ds(l, 1), :]
            b = jnp.concatenate([b, b], axis=1)
            b = jnp.concatenate([b, b], axis=1)
            nxt = jnp.minimum(l + 1, LAYERS - 1)
            rs, ss = [], []
            for g in range(BY // 8):
                cols = [ubuf[l, xq + i, pl.ds(8 * g, WIN)].reshape(WIN * ZL, LANES) for i in range(QUAD)]
                rs.append(jnp.dot(ty[...], jnp.concatenate(cols, axis=1), preferred_element_type=F32).astype(BF16))
            for g in range(BY // 8):
                zs = []
                for i in range(QUAD):
                    u = rs[g][:, LANES * i:LANES * (i + 1)].reshape(4, 2, ZL, LANES)
                    ya, yb = u[:, 0], u[:, 1]
                    lo = jnp.concatenate([ya[:, :, :C], yb[:, :, :C]], axis=2)
                    hi = jnp.concatenate([ya[:, :, C:], yb[:, :, C:]], axis=2)
                    zs.append(jnp.concatenate([lo, hi], axis=1).reshape(4 * BZ, LANES))
                dz = jnp.concatenate([jnp.concatenate(zs[:2], axis=0), jnp.concatenate(zs[2:], axis=0)], axis=1)
                ss.append(jnp.dot(tz[...], dz, preferred_element_type=F32).astype(BF16))
            for g in range(BY // 8):
                lhs = []
                for h in range(2):
                    sh = ss[g][:, LANES * h:LANES * (h + 1)].reshape(8, 2, ZL, LANES)
                    lhs.append(jnp.concatenate([sh[:, 0], sh[:, 1]], axis=2).reshape(8 * ZL, 2 * LANES))
                m = jnp.dot(jnp.concatenate(lhs, axis=0), w4[...], preferred_element_type=F32) + b
                m = jax.nn.gelu(m, approximate=True)
                for i in range(QUAD):
                    mi = m[64 * i:64 * (i + 1)].reshape(4, 1, ZL, 2 * LANES)
                    mi = jnp.concatenate([mi[..., :LANES], mi[..., LANES:]], axis=1).reshape(8, ZL, LANES)
                    old = vbuf[l, own + xq + i, pl.ds(8 * g, 8)].astype(F32)
                    vbuf[nxt, own + xq + i, pl.ds(8 * g, 8)] = (old + mi).astype(BF16)

    def zero_planes(l):
        vbuf[l, pl.ds(own + x_of(NCH - 1), CH)] = jnp.zeros((CH, BY, ZL, LANES), BF16)

    def zero_halo(y0):
        def body(n, carry):
            ubuf[n // BX, n % BX, pl.ds(y0, H)] = jnp.zeros((H, ZL, LANES), BF16)
            return carry

        lax.fori_loop(0, LAYERS * BX, body, 0)

    def pack(k, seg):
        with jax.named_scope("pack"):
            load(k, seg).wait()
            x0 = x_of(k)
            ys = pl.ds(*SEGS[seg])

            def body(p, c):
                s = stage[k, p, ys]
                vbuf[0, own + x0 + p, ys] = jnp.concatenate([s[:, :ZL], s[:, ZL:]], axis=2)
                return c

            lax.fori_loop(0, CH, body, 0)

    def pack_all(seg, n):
        def body(k, c):
            pack(k, seg)
            return c

        lax.fori_loop(0, n, body, 0)

    with jax.named_scope("zero0"):
        zero_planes(0)
    x_mat(0, 0)
    pack_all(0, NCH - 1)
    x_seg(0, 0, 0)
    pl.semaphore_wait(barrier, 3)
    y_send(0, 0, 0)
    pack_all(1, NCH - 1)
    x_seg(0, 0, 1)
    y_send(0, 0, 1)
    pack(NCH - 1, 0)
    pack(NCH - 1, 1)
    pack_all(2, NCH)
    x_copy(0).start()
    x_seg(0, 0, 2)
    for l in range(1, LAYERS):
        zero_planes(l)

    @pl.when(jnp.logical_not(has_left))
    def _():
        zero_halo(0)

    @pl.when(jnp.logical_not(has_right))
    def _():
        zero_halo(H + BY)

    def layer(l, carry):
        def xs(k, c):
            @pl.when(k == 2)
            def _():
                with jax.named_scope("xwait"):
                    x_copy(l).wait()

            x_pass(l, k)
            return c

        lax.fori_loop(1, NCH, xs, 0)
        with jax.named_scope("mats"):
            layer_mats(l)

        def ys(q, c):
            @pl.when((q == NQ - CH // QUAD) & (l < LAYERS - 1))
            def _():
                x_pass(l + 1, 0)

            y_quad(l, q)

            @pl.when(l == LAYERS - 1)
            def _():
                store(q).start()

            return c

        lax.fori_loop(0, NQ, ys, 0)

        @pl.when(l < LAYERS - 1)
        def _():
            x_copy(l + 1).start()

        return carry

    def store(q):
        xs = xq_of(q)
        return pltpu.make_async_copy(vbuf.at[LAYERS - 1, pl.ds(own + xs, QUAD)], out.at[pl.ds(xs, QUAD)], out_sem.at[q])

    lax.fori_loop(0, LAYERS, layer, 0)

    def finish(n, carry):
        l, q = n // NQ, n % NQ

        @pl.when(has_left)
        def _():
            y_copy(l, q, 0).wait_send()

        @pl.when(has_right)
        def _():
            y_copy(l, q, 1).wait_send()

        return carry

    with jax.named_scope("finish"):
        lax.fori_loop(0, LAYERS * NQ, finish, 0)
        for q in range(NQ):
            store(q).wait()


def unpack_kernel(src, dst):
    s = src[...]
    dst[:, :, :ZL, :] = s[:, :, :, :C]
    dst[:, :, ZL:, :] = s[:, :, :, C:]


def solution(mesh):
    y_count = mesh.shape[COL_AXIS]
    vol_spec = P(PARTS_AXIS, ROW_AXIS, COL_AXIS, None)
    any_spec = pl.BlockSpec(memory_space=pl.ANY)
    vmem_spec = pl.BlockSpec(memory_space=pltpu.VMEM)

    def local_layers(volume, filter_taps, mix_weights, mix_bias):
        vol = jnp.transpose(volume, (1, 2, 3, 0))
        packed = pl.pallas_call(
            functools.partial(kernel, y_count),
            out_shape=jax.ShapeDtypeStruct((BX, BY, ZL, LANES), BF16),
            in_specs=[any_spec, pl.BlockSpec(memory_space=pltpu.SMEM), vmem_spec, vmem_spec],
            out_specs=any_spec,
            scratch_shapes=[
                pltpu.VMEM((NCH, CH, BY, BZ, C), BF16),
                pltpu.VMEM((LAYERS, XS, BY, ZL, LANES), BF16),
                pltpu.VMEM((LAYERS, BX, YS, ZL, LANES), BF16),
                pltpu.VMEM((CH * ZL, WIN * ZL), BF16),
                pltpu.VMEM((CH * ZL, WIN * ZL), BF16),
                pltpu.VMEM((8 * BZ, 8 * BZ), BF16),
                pltpu.VMEM((4 * C, 4 * C), BF16),
                pltpu.SemaphoreType.DMA((NCH, 3)),
                pltpu.SemaphoreType.DMA((NQ,)),
                pltpu.SemaphoreType.DMA((LAYERS, NQ, 2)),
                pltpu.SemaphoreType.DMA((LAYERS, NQ, 2)),
                pltpu.SemaphoreType.DMA((LAYERS,)),
                pltpu.SemaphoreType.DMA((LAYERS,)),
            ],
            compiler_params=pltpu.CompilerParams(collective_id=0, has_side_effects=True, vmem_limit_bytes=60 * 2**20),
        )(vol, filter_taps, mix_weights, mix_bias)
        result = pl.pallas_call(
            unpack_kernel,
            grid=(8,),
            out_shape=jax.ShapeDtypeStruct((BX, BY, BZ, C), BF16),
            in_specs=[pl.BlockSpec((BX // 8, BY, ZL, LANES), lambda i: (i, 0, 0, 0))],
            out_specs=pl.BlockSpec((BX // 8, BY, BZ, C), lambda i: (i, 0, 0, 0)),
        )(packed)
        return jnp.transpose(result, (3, 0, 1, 2))

    return jax.shard_map(local_layers, mesh=mesh, in_specs=(vol_spec, P(), P(), P()), out_specs=vol_spec, check_vma=False)
```

time: 126 us -> 109 us (0.87)
  Pallas kernels: 124 us -> 108 us
  local copies, waits for them, and re-layouts: 1.3 us -> 0 us
    pallas_call x1, Pallas kernels: 116 us -> 99.9 us  [local_layers(): pl.pallas_call(functools.partial(kernel, y_count), out_shape=jax.ShapeDty...]
    reshape x1 -> x0, local copies, waits for them, and re-layouts: 1.3 us -> none  [local_layers(): taps = filter_taps.reshape(LAYERS * 3, TAPS)]
where the time goes in v2:
time: 109 us; the launch traced here: 108 us
  Pallas kernels  108 us (99%)
    pallas_call x1, Pallas kernels, local_layers(): pl.pallas_call(functools.partial(kernel, y_count), out_shape=jax.ShapeDty...  99.9 us
    pallas_call x1, Pallas kernels, local_layers(): pl.pallas_call(unpack_kernel, grid=(8,), out_shape=jax.ShapeDtypeStruct((...  8.31 us

profile of v2, /device:TPU:96, one launch (start us, length us, event | category | flops | bytes accessed | tf_op | source)
XLA Modules:
  0.0 108.3 jit_solution(11134559668396121271)
XLA Ops:
  0.0 99.9 %shard_map.46.src = bf16[32,32,16,128]{3,2,1,0:T(8,128)(2,1)} custom-call(bf16[32,32,32,64]{3,2,1,0:T(8,128)(2,1)} %bitcast.2, f32[3,3,21]{2,1,0:T(4,128)} %taps.1, bf16[3,64,64]{2,1,0:T(8,128)(2,1)} %wmat.1, f32[3,64]{1,0:T(4,128)} %bias.1), custom_call_target="tpu_custom_call" | custom-call | tf_op jit(solution)/shard_map/pallas_call | solution.py:315
  100.0 8.3 %shard_map.47 = bf16[32,32,32,64]{3,2,1,0:T(8,128)(2,1)} custom-call(bf16[32,32,16,128]{3,2,1,0:T(8,128)(2,1)} %shard_map.46.src), custom_call_target="tpu_custom_call" | custom-call | tf_op jit(solution)/shard_map/pallas_call | solution.py:337

commit v3 on v2

--- a/solution.py
+++ b/solution.py
@@ -23,6 +23,7 @@
 NCH = BX // CH
 QUAD = 4
 NQ = BX // QUAD
+PART = 4
 WIN = CH + 2 * H
 XS = BX + H
 YS = BY + 2 * H
@@ -203,7 +204,7 @@
                 vbuf[0, own + x0 + p, ys] = jnp.concatenate([s[:, :ZL], s[:, ZL:]], axis=2)
                 return c
 
-            lax.fori_loop(0, CH, body, 0)
+            lax.fori_loop(0, CH, body, 0, unroll=True)
 
     def pack_all(seg, n):
         def body(k, c):
@@ -298,10 +299,30 @@
             store(q).wait()
 
 
-def unpack_kernel(src, dst):
-    s = src[...]
-    dst[:, :, :ZL, :] = s[:, :, :, :C]
-    dst[:, :, ZL:, :] = s[:, :, :, C:]
+def unpack_kernel(src, dst, got, buf, in_sems, out_sems):
+    def read(p):
+        xs = pl.ds(p * PART, PART)
+        return pltpu.make_async_copy(src.at[xs], got.at[xs], in_sems.at[p])
+
+    def write(p):
+        xs = pl.ds(p * PART, PART)
+        return pltpu.make_async_copy(buf.at[xs], dst.at[xs], out_sems.at[p])
+
+    for p in range(BX // PART):
+        read(p).start()
+
+    def body(p, carry):
+        xs = pl.ds(p * PART, PART)
+        read(p).wait()
+        s = got[xs]
+        buf[xs, :, :ZL, :] = s[:, :, :, :C]
+        buf[xs, :, ZL:, :] = s[:, :, :, C:]
+        write(p).start()
+        return carry
+
+    lax.fori_loop(0, BX // PART, body, 0)
+    for p in range(BX // PART):
+        write(p).wait()
 
 
 def solution(mesh):
@@ -336,10 +357,16 @@
         )(vol, filter_taps, mix_weights, mix_bias)
         result = pl.pallas_call(
             unpack_kernel,
-            grid=(8,),
             out_shape=jax.ShapeDtypeStruct((BX, BY, BZ, C), BF16),
-            in_specs=[pl.BlockSpec((BX // 8, BY, ZL, LANES), lambda i: (i, 0, 0, 0))],
-            out_specs=pl.BlockSpec((BX // 8, BY, BZ, C), lambda i: (i, 0, 0, 0)),
+            in_specs=[any_spec],
+            out_specs=any_spec,
+            scratch_shapes=[
+                pltpu.VMEM((BX, BY, ZL, LANES), BF16),
+                pltpu.VMEM((BX, BY, BZ, C), BF16),
+                pltpu.SemaphoreType.DMA((BX // PART,)),
+                pltpu.SemaphoreType.DMA((BX // PART,)),
+            ],
+            compiler_params=pltpu.CompilerParams(vmem_limit_bytes=60 * 2**20),
         )(packed)
         return jnp.transpose(result, (3, 0, 1, 2))
 

time: 109 us -> 104 us (0.954); the launches traced: 108 us -> 102 us
  Pallas kernels: 108 us -> 102 us
    pallas_call x1, Pallas kernels: 8.31 us -> 4.85 us  [local_layers(): pl.pallas_call(unpack_kernel, out_shape=jax.ShapeDtypeStruct((BX, BY, BZ,...]
    pallas_call x1, Pallas kernels: 99.9 us -> 97.2 us  [local_layers(): pl.pallas_call(functools.partial(kernel, y_count), out_shape=jax.ShapeDty...]
where the time goes in v3:
time: 104 us; the launch traced here: 102 us
  Pallas kernels  102 us (98%)
    pallas_call x1, Pallas kernels, local_layers(): pl.pallas_call(functools.partial(kernel, y_count), out_shape=jax.ShapeDty...  97.2 us
    pallas_call x1, Pallas kernels, local_layers(): pl.pallas_call(unpack_kernel, out_shape=jax.ShapeDtypeStruct((BX, BY, BZ,...  4.85 us

profile of v3, /device:TPU:96, one launch (start us, length us, event | category | flops | bytes accessed | tf_op | source)
XLA Modules:
  0.0 102.1 jit_solution(13960275030822690576)
XLA Ops:
  0.0 97.2 %shard_map.46.src = bf16[32,32,16,128]{3,2,1,0:T(8,128)(2,1)} custom-call(bf16[32,32,32,64]{3,2,1,0:T(8,128)(2,1)} %bitcast.2, f32[3,3,21]{2,1,0:T(4,128)} %taps.1, bf16[3,64,64]{2,1,0:T(8,128)(2,1)} %wmat.1, f32[3,64]{1,0:T(4,128)} %bias.1), custom_call_target="tpu_custom_call" | custom-call | tf_op jit(solution)/shard_map/pallas_call | solution.py:336
  97.2 4.9 %shard_map.47 = bf16[32,32,32,64]{3,2,1,0:T(8,128)(2,1)} custom-call(bf16[32,32,16,128]{3,2,1,0:T(8,128)(2,1)} %shard_map.46.src), custom_call_target="tpu_custom_call" | custom-call | tf_op jit(solution)/shard_map/pallas_call | solution.py:358

commit v4 on v3

--- a/solution.py
+++ b/solution.py
@@ -25,6 +25,7 @@
 NQ = BX // QUAD
 PART = 4
 WIN = CH + 2 * H
+HEAD = CH + H
 XS = BX + H
 YS = BY + 2 * H
 SEGS = ((0, H), (BY - H, H), (H, BY - 2 * H))
@@ -42,7 +43,7 @@
     return jnp.where(i % inner == j % inner, acc, 0.0).astype(BF16)
 
 
-def kernel(y_count, vol, taps, wmat, bias, out, stage, vbuf, ubuf, tx, ty, tz, w4, in_sem, out_sem, ysend, yrecv, xsend, xrecv):
+def kernel(y_count, vol, taps_hbm, wmat_hbm, bias_hbm, out, stage, vbuf, ubuf, tx, ty, tz, w4, taps, wmat, bias, in_sem, small_sem, out_sem, ysend, yrecv, xsend, xrecv):
     xi = lax.axis_index(ROW_AXIS)
     yi = lax.axis_index(COL_AXIS)
     own = xi * H
@@ -57,29 +58,44 @@
     def xq_of(q):
         return jnp.where(xi == 0, QUAD * q, BX - QUAD - QUAD * q)
 
-    def load(k, seg):
-        ys = pl.ds(*SEGS[seg])
-        return pltpu.make_async_copy(vol.at[pl.ds(x_of(k), CH), ys], stage.at[k, :, ys], in_sem.at[k, seg])
-
-    for seg in range(2):
-        for k in range(NCH - 1):
-            load(k, seg).start()
-    load(NCH - 1, 0).start()
-    load(NCH - 1, 1).start()
-    for k in range(NCH):
-        load(k, 2).start()
+    x_head = jnp.where(xi == 0, 0, BX - HEAD)
+    x_rest = jnp.where(xi == 0, HEAD, 0)
+
+    def load(n):
+        xs = pl.ds(x_rest, BX - HEAD) if n == 2 else pl.ds(x_head, HEAD)
+        ys = pl.ds(0, BY) if n == 2 else pl.ds(*SEGS[min(n, 2)])
+        return pltpu.make_async_copy(vol.at[xs, ys], stage.at[xs, ys], in_sem.at[n])
+
+    small = [
+        pltpu.make_async_copy(taps_hbm, taps, small_sem.at[0]),
+        pltpu.make_async_copy(wmat_hbm, wmat, small_sem.at[1]),
+        pltpu.make_async_copy(bias_hbm, bias, small_sem.at[2]),
+    ]
+    small[0].start()
+    for n in range(4):
+        load(n).start()
+    small[1].start()
+    small[2].start()
 
     barrier = pltpu.get_barrier_semaphore()
-    pl.semaphore_signal(barrier, inc=1, device_id={COL_AXIS: left})
-    pl.semaphore_signal(barrier, inc=1, device_id={COL_AXIS: right})
+
+    @pl.when(has_left)
+    def _():
+        pl.semaphore_signal(barrier, inc=1, device_id={COL_AXIS: left})
+
+    @pl.when(has_right)
+    def _():
+        pl.semaphore_signal(barrier, inc=1, device_id={COL_AXIS: right})
+
     pl.semaphore_signal(barrier, inc=1, device_id={ROW_AXIS: 1 - xi})
+    neighbours = 1 + has_left.astype(jnp.int32) + has_right.astype(jnp.int32)
 
     def y_copy(l, q, side):
         xs = pl.ds(xq_of(q), QUAD)
         src = ubuf.at[l, xs, pl.ds(H, H)] if side == 0 else ubuf.at[l, xs, pl.ds(BY, H)]
         dst = ubuf.at[l, xs, pl.ds(H + BY, H)] if side == 0 else ubuf.at[l, xs, pl.ds(0, H)]
         return pltpu.make_async_remote_copy(
-            src_ref=src, dst_ref=dst, send_sem=ysend.at[l, q, side], recv_sem=yrecv.at[l, q, side],
+            src_ref=src, dst_ref=dst, send_sem=ysend.at[side], recv_sem=yrecv.at[l, q],
             device_id={COL_AXIS: left if side == 0 else right})
 
     def x_copy(l):
@@ -142,11 +158,15 @@
 
     def y_quad(l, q):
         with jax.named_scope("ywait"):
-            @pl.when(has_left)
-            def _():
-                y_copy(l, q, 1).wait_recv()
-
-            @pl.when(has_right)
+            both = ubuf.at[l, pl.ds(xq_of(q), QUAD), pl.ds(0, 2 * H)]
+
+            @pl.when(has_left & has_right)
+            def _():
+                pltpu.make_async_remote_copy(
+                    src_ref=both, dst_ref=both, send_sem=ysend.at[0], recv_sem=yrecv.at[l, q],
+                    device_id={COL_AXIS: left}).wait_recv()
+
+            @pl.when(jnp.logical_not(has_left & has_right))
             def _():
                 y_copy(l, q, 0).wait_recv()
 
@@ -186,58 +206,51 @@
     def zero_planes(l):
         vbuf[l, pl.ds(own + x_of(NCH - 1), CH)] = jnp.zeros((CH, BY, ZL, LANES), BF16)
 
-    def zero_halo(y0):
+    def zero_halo(l, y0):
         def body(n, carry):
-            ubuf[n // BX, n % BX, pl.ds(y0, H)] = jnp.zeros((H, ZL, LANES), BF16)
+            ubuf[l, n, pl.ds(y0, H)] = jnp.zeros((H, ZL, LANES), BF16)
             return carry
 
-        lax.fori_loop(0, LAYERS * BX, body, 0)
-
-    def pack(k, seg):
+        lax.fori_loop(0, BX, body, 0)
+
+    def pack(n, x0, count, first, ny):
         with jax.named_scope("pack"):
-            load(k, seg).wait()
-            x0 = x_of(k)
-            ys = pl.ds(*SEGS[seg])
+            ys = pl.ds(first, ny)
 
             def body(p, c):
-                s = stage[k, p, ys]
+                s = stage[x0 + p, ys]
                 vbuf[0, own + x0 + p, ys] = jnp.concatenate([s[:, :ZL], s[:, ZL:]], axis=2)
                 return c
 
-            lax.fori_loop(0, CH, body, 0, unroll=True)
-
-    def pack_all(seg, n):
-        def body(k, c):
-            pack(k, seg)
-            return c
-
-        lax.fori_loop(0, n, body, 0)
+            lax.fori_loop(0, count, body, 0, unroll=True)
 
     with jax.named_scope("zero0"):
-        zero_planes(0)
+        for seg in range(2):
+            first, ny = SEGS[seg]
+            pad = WIN - HEAD
+            vbuf[0, pl.ds(own + jnp.where(xi == 0, HEAD, BX - WIN), pad), pl.ds(first, ny)] = jnp.zeros((pad, ny, ZL, LANES), BF16)
+    small[0].wait()
     x_mat(0, 0)
-    pack_all(0, NCH - 1)
+    load(0).wait()
+    pack(0, x_head, HEAD, *SEGS[0])
     x_seg(0, 0, 0)
-    pl.semaphore_wait(barrier, 3)
+    with jax.named_scope("barrier"):
+        pl.semaphore_wait(barrier, neighbours)
     y_send(0, 0, 0)
-    pack_all(1, NCH - 1)
+    load(1).wait()
+    pack(1, x_head, HEAD, *SEGS[1])
     x_seg(0, 0, 1)
     y_send(0, 0, 1)
-    pack(NCH - 1, 0)
-    pack(NCH - 1, 1)
-    pack_all(2, NCH)
+    load(2).wait()
+    pack(2, x_rest, BX - HEAD, 0, BY)
     x_copy(0).start()
+    load(3).wait()
+    pack(3, x_head, HEAD, *SEGS[2])
     x_seg(0, 0, 2)
     for l in range(1, LAYERS):
         zero_planes(l)
-
-    @pl.when(jnp.logical_not(has_left))
-    def _():
-        zero_halo(0)
-
-    @pl.when(jnp.logical_not(has_right))
-    def _():
-        zero_halo(H + BY)
+    small[1].wait()
+    small[2].wait()
 
     def layer(l, carry):
         def xs(k, c):
@@ -253,6 +266,14 @@
         with jax.named_scope("mats"):
             layer_mats(l)
 
+        @pl.when(jnp.logical_not(has_left))
+        def _():
+            zero_halo(l, 0)
+
+        @pl.when(jnp.logical_not(has_right))
+        def _():
+            zero_halo(l, H + BY)
+
         def ys(q, c):
             @pl.when((q == NQ - CH // QUAD) & (l < LAYERS - 1))
             def _():
@@ -276,37 +297,31 @@
 
     def store(q):
         xs = xq_of(q)
-        return pltpu.make_async_copy(vbuf.at[LAYERS - 1, pl.ds(own + xs, QUAD)], out.at[pl.ds(xs, QUAD)], out_sem.at[q])
+        return pltpu.make_async_copy(vbuf.at[LAYERS - 1, pl.ds(own + xs, QUAD)], out.at[pl.ds(xs, QUAD)], out_sem)
 
     lax.fori_loop(0, LAYERS, layer, 0)
 
-    def finish(n, carry):
-        l, q = n // NQ, n % NQ
-
-        @pl.when(has_left)
-        def _():
-            y_copy(l, q, 0).wait_send()
-
-        @pl.when(has_right)
-        def _():
-            y_copy(l, q, 1).wait_send()
-
-        return carry
-
     with jax.named_scope("finish"):
-        lax.fori_loop(0, LAYERS * NQ, finish, 0)
-        for q in range(NQ):
-            store(q).wait()
-
-
-def unpack_kernel(src, dst, got, buf, in_sems, out_sems):
+        for side in range(2):
+            sent = ubuf.at[:, :, pl.ds(0, H)]
+
+            @pl.when(has_left if side == 0 else has_right)
+            def _():
+                pltpu.make_async_remote_copy(
+                    src_ref=sent, dst_ref=sent, send_sem=ysend.at[side], recv_sem=yrecv.at[0, 0],
+                    device_id={COL_AXIS: left if side == 0 else right}).wait_send()
+
+        pltpu.make_async_copy(vbuf.at[LAYERS - 1, pl.ds(own, BX)], out, out_sem).wait()
+
+
+def unpack_kernel(src, dst, got, buf, in_sems, out_sem):
     def read(p):
         xs = pl.ds(p * PART, PART)
         return pltpu.make_async_copy(src.at[xs], got.at[xs], in_sems.at[p])
 
     def write(p):
         xs = pl.ds(p * PART, PART)
-        return pltpu.make_async_copy(buf.at[xs], dst.at[xs], out_sems.at[p])
+        return pltpu.make_async_copy(buf.at[xs], dst.at[xs], out_sem)
 
     for p in range(BX // PART):
         read(p).start()
@@ -321,35 +336,37 @@
         return carry
 
     lax.fori_loop(0, BX // PART, body, 0)
-    for p in range(BX // PART):
-        write(p).wait()
+    pltpu.make_async_copy(buf, dst, out_sem).wait()
 
 
 def solution(mesh):
     y_count = mesh.shape[COL_AXIS]
     vol_spec = P(PARTS_AXIS, ROW_AXIS, COL_AXIS, None)
     any_spec = pl.BlockSpec(memory_space=pl.ANY)
-    vmem_spec = pl.BlockSpec(memory_space=pltpu.VMEM)
 
     def local_layers(volume, filter_taps, mix_weights, mix_bias):
         vol = jnp.transpose(volume, (1, 2, 3, 0))
         packed = pl.pallas_call(
             functools.partial(kernel, y_count),
             out_shape=jax.ShapeDtypeStruct((BX, BY, ZL, LANES), BF16),
-            in_specs=[any_spec, pl.BlockSpec(memory_space=pltpu.SMEM), vmem_spec, vmem_spec],
+            in_specs=[any_spec] * 4,
             out_specs=any_spec,
             scratch_shapes=[
-                pltpu.VMEM((NCH, CH, BY, BZ, C), BF16),
+                pltpu.VMEM((BX, BY, BZ, C), BF16),
                 pltpu.VMEM((LAYERS, XS, BY, ZL, LANES), BF16),
                 pltpu.VMEM((LAYERS, BX, YS, ZL, LANES), BF16),
                 pltpu.VMEM((CH * ZL, WIN * ZL), BF16),
                 pltpu.VMEM((CH * ZL, WIN * ZL), BF16),
                 pltpu.VMEM((8 * BZ, 8 * BZ), BF16),
                 pltpu.VMEM((4 * C, 4 * C), BF16),
-                pltpu.SemaphoreType.DMA((NCH, 3)),
-                pltpu.SemaphoreType.DMA((NQ,)),
-                pltpu.SemaphoreType.DMA((LAYERS, NQ, 2)),
-                pltpu.SemaphoreType.DMA((LAYERS, NQ, 2)),
+                pltpu.SMEM((LAYERS, 3, TAPS), F32),
+                pltpu.VMEM((LAYERS, C, C), BF16),
+                pltpu.VMEM((LAYERS, C), F32),
+                pltpu.SemaphoreType.DMA((4,)),
+                pltpu.SemaphoreType.DMA((3,)),
+                pltpu.SemaphoreType.DMA,
+                pltpu.SemaphoreType.DMA((2,)),
+                pltpu.SemaphoreType.DMA((LAYERS, NQ)),
                 pltpu.SemaphoreType.DMA((LAYERS,)),
                 pltpu.SemaphoreType.DMA((LAYERS,)),
             ],
@@ -364,7 +381,7 @@
                 pltpu.VMEM((BX, BY, ZL, LANES), BF16),
                 pltpu.VMEM((BX, BY, BZ, C), BF16),
                 pltpu.SemaphoreType.DMA((BX // PART,)),
-                pltpu.SemaphoreType.DMA((BX // PART,)),
+                pltpu.SemaphoreType.DMA,
             ],
             compiler_params=pltpu.CompilerParams(vmem_limit_bytes=60 * 2**20),
         )(packed)

time: 104 us -> 100 us (0.962); the launches traced: 102 us -> 100 us
  Pallas kernels: 102 us -> 100 us
    pallas_call x1, Pallas kernels: 97.2 us -> 95.6 us  [local_layers(): pl.pallas_call(functools.partial(kernel, y_count), out_shape=jax.ShapeDty...]
where the time goes in v4:
time: 100 us
  Pallas kernels  100 us (100%)
    pallas_call x1, Pallas kernels, local_layers(): pl.pallas_call(functools.partial(kernel, y_count), out_shape=jax.ShapeDty...  95.6 us
    pallas_call x1, Pallas kernels, local_layers(): pl.pallas_call(unpack_kernel, out_shape=jax.ShapeDtypeStruct((BX, BY, BZ,...  4.79 us

profile of v4, /device:TPU:96, one launch (start us, length us, event | category | flops | bytes accessed | tf_op | source)
XLA Modules:
  0.0 100.4 jit_solution(18391258742380750266)
XLA Ops:
  0.0 95.6 %shard_map.46.src = bf16[32,32,16,128]{3,2,1,0:T(8,128)(2,1)} custom-call(bf16[32,32,32,64]{3,2,1,0:T(8,128)(2,1)} %bitcast.2, f32[3,3,21]{2,1,0:T(4,128)} %taps_hbm.1, bf16[3,64,64]{2,1,0:T(8,128)(2,1)} %wmat_hbm.1, f32[3,64]{1,0:T(4,128)} %bias_hbm.1), custom_call_target="tpu_custom_call" | custom-call | tf_op jit(solution)/shard_map/pallas_call | solution.py:349
  95.6 4.8 %shard_map.47 = bf16[32,32,32,64]{3,2,1,0:T(8,128)(2,1)} custom-call(bf16[32,32,16,128]{3,2,1,0:T(8,128)(2,1)} %shard_map.46.src), custom_call_target="tpu_custom_call" | custom-call | tf_op jit(solution)/shard_map/pallas_call | solution.py:375

commit v5 on v4

--- a/solution.py
+++ b/solution.py
@@ -23,12 +23,11 @@
 NCH = BX // CH
 QUAD = 4
 NQ = BX // QUAD
-PART = 4
 WIN = CH + 2 * H
 HEAD = CH + H
 XS = BX + H
 YS = BY + 2 * H
-SEGS = ((0, H), (BY - H, H), (H, BY - 2 * H))
+SEGS = ((BY - H, H), (0, H), (H, BY - 2 * H))
 F32 = jnp.float32
 BF16 = jnp.bfloat16
 
@@ -43,7 +42,37 @@
     return jnp.where(i % inner == j % inner, acc, 0.0).astype(BF16)
 
 
-def kernel(y_count, vol, taps_hbm, wmat_hbm, bias_hbm, out, stage, vbuf, ubuf, tx, ty, tz, w4, taps, wmat, bias, in_sem, small_sem, out_sem, ysend, yrecv, xsend, xrecv):
+def y_compute(window_of, old, put, ty, tz, w4, b):
+    b = jnp.concatenate([b, b], axis=1)
+    b = jnp.concatenate([b, b], axis=1)
+    rs, ss = [], []
+    for g in range(BY // 8):
+        cols = [window_of(i, 8 * g).reshape(WIN * ZL, LANES) for i in range(QUAD)]
+        rs.append(jnp.dot(ty[...], jnp.concatenate(cols, axis=1), preferred_element_type=F32).astype(BF16))
+    for g in range(BY // 8):
+        zs = []
+        for i in range(QUAD):
+            u = rs[g][:, LANES * i:LANES * (i + 1)].reshape(4, 2, ZL, LANES)
+            ya, yb = u[:, 0], u[:, 1]
+            lo = jnp.concatenate([ya[:, :, :C], yb[:, :, :C]], axis=2)
+            hi = jnp.concatenate([ya[:, :, C:], yb[:, :, C:]], axis=2)
+            zs.append(jnp.concatenate([lo, hi], axis=1).reshape(4 * BZ, LANES))
+        dz = jnp.concatenate([jnp.concatenate(zs[:2], axis=0), jnp.concatenate(zs[2:], axis=0)], axis=1)
+        ss.append(jnp.dot(tz[...], dz, preferred_element_type=F32).astype(BF16))
+    for g in range(BY // 8):
+        lhs = []
+        for h in range(2):
+            sh = ss[g][:, LANES * h:LANES * (h + 1)].reshape(8, 2, ZL, LANES)
+            lhs.append(jnp.concatenate([sh[:, 0], sh[:, 1]], axis=2).reshape(8 * ZL, 2 * LANES))
+        m = jnp.dot(jnp.concatenate(lhs, axis=0), w4[...], preferred_element_type=F32) + b
+        m = jax.nn.gelu(m, approximate=True)
+        for i in range(QUAD):
+            mi = m[64 * i:64 * (i + 1)].reshape(4, 1, ZL, 2 * LANES)
+            mi = jnp.concatenate([mi[..., :LANES], mi[..., LANES:]], axis=1).reshape(8, ZL, LANES)
+            put(i, 8 * g, (old(i, 8 * g).astype(F32) + mi).astype(BF16))
+
+
+def kernel(y_count, vol, taps_hbm, wmat_hbm, bias_hbm, out, u_out, ty_out, tz_out, w4_out, stage, vbuf, ubuf, tx, ty, tz, w4, taps, wmat, bias, in_sem, small_sem, out_sem, ysend, yrecv, xsend, xrecv):
     xi = lax.axis_index(ROW_AXIS)
     yi = lax.axis_index(COL_AXIS)
     own = xi * H
@@ -124,18 +153,33 @@
             for i in range(count):
                 ubuf[l, pl.ds(x0, CH), H + first + i] = r[:, LANES * i:LANES * (i + 1)].reshape(CH, ZL, LANES)
 
+    def last_copy(side):
+        l, q = LAYERS - 1, NQ - 1
+        src = ubuf.at[l, pl.ds(xq_of(q), QUAD), pl.ds(H if side == 0 else BY, H)]
+        return pltpu.make_async_remote_copy(
+            src_ref=src, dst_ref=u_out.at[:, pl.ds(H + BY if side == 0 else 0, H)], send_sem=ysend.at[side], recv_sem=yrecv.at[l, q],
+            device_id={COL_AXIS: left if side == 0 else right})
+
     def y_send(l, k, side):
-        @pl.when(has_left if side == 0 else has_right)
-        def _():
-            for j in range(CH // QUAD):
-                y_copy(l, k * (CH // QUAD) + j, side).start()
+        goes = has_left if side == 0 else has_right
+        for j in range(CH // QUAD):
+            q = k * (CH // QUAD) + j
+            last = (l == LAYERS - 1) & (q == NQ - 1)
+
+            @pl.when(goes & jnp.logical_not(last))
+            def _():
+                y_copy(l, q, side).start()
+
+            @pl.when(goes & last)
+            def _():
+                last_copy(side).start()
 
     def x_pass(l, k):
         x_mat(l, k)
         x_seg(l, k, 0)
+        y_send(l, k, 1)
+        x_seg(l, k, 1)
         y_send(l, k, 0)
-        x_seg(l, k, 1)
-        y_send(l, k, 1)
         x_seg(l, k, 2)
 
     def layer_mats(l):
@@ -156,7 +200,7 @@
         keep = (i // 2 == j % 2) & (i % 2 == j // 2)
         w4[...] = jnp.where(keep, w, 0.0).astype(BF16)
 
-    def y_quad(l, q):
+    def y_wait(l, q):
         with jax.named_scope("ywait"):
             both = ubuf.at[l, pl.ds(xq_of(q), QUAD), pl.ds(0, 2 * H)]
 
@@ -170,38 +214,22 @@
             def _():
                 y_copy(l, q, 0).wait_recv()
 
+    def y_quad(l, q):
+        y_wait(l, q)
         with jax.named_scope("yquad"):
             xq = xq_of(q)
-            b = bias[pl.ds(l, 1), :]
-            b = jnp.concatenate([b, b], axis=1)
-            b = jnp.concatenate([b, b], axis=1)
             nxt = jnp.minimum(l + 1, LAYERS - 1)
-            rs, ss = [], []
-            for g in range(BY // 8):
-                cols = [ubuf[l, xq + i, pl.ds(8 * g, WIN)].reshape(WIN * ZL, LANES) for i in range(QUAD)]
-                rs.append(jnp.dot(ty[...], jnp.concatenate(cols, axis=1), preferred_element_type=F32).astype(BF16))
-            for g in range(BY // 8):
-                zs = []
-                for i in range(QUAD):
-                    u = rs[g][:, LANES * i:LANES * (i + 1)].reshape(4, 2, ZL, LANES)
-                    ya, yb = u[:, 0], u[:, 1]
-                    lo = jnp.concatenate([ya[:, :, :C], yb[:, :, :C]], axis=2)
-                    hi = jnp.concatenate([ya[:, :, C:], yb[:, :, C:]], axis=2)
-                    zs.append(jnp.concatenate([lo, hi], axis=1).reshape(4 * BZ, LANES))
-                dz = jnp.concatenate([jnp.concatenate(zs[:2], axis=0), jnp.concatenate(zs[2:], axis=0)], axis=1)
-                ss.append(jnp.dot(tz[...], dz, preferred_element_type=F32).astype(BF16))
-            for g in range(BY // 8):
-                lhs = []
-                for h in range(2):
-                    sh = ss[g][:, LANES * h:LANES * (h + 1)].reshape(8, 2, ZL, LANES)
-                    lhs.append(jnp.concatenate([sh[:, 0], sh[:, 1]], axis=2).reshape(8 * ZL, 2 * LANES))
-                m = jnp.dot(jnp.concatenate(lhs, axis=0), w4[...], preferred_element_type=F32) + b
-                m = jax.nn.gelu(m, approximate=True)
-                for i in range(QUAD):
-                    mi = m[64 * i:64 * (i + 1)].reshape(4, 1, ZL, 2 * LANES)
-                    mi = jnp.concatenate([mi[..., :LANES], mi[..., LANES:]], axis=1).reshape(8, ZL, LANES)
-                    old = vbuf[l, own + xq + i, pl.ds(8 * g, 8)].astype(F32)
-                    vbuf[nxt, own + xq + i, pl.ds(8 * g, 8)] = (old + mi).astype(BF16)
+
+            def window_of(i, y0):
+                return ubuf[l, xq + i, pl.ds(y0, WIN)]
+
+            def old(i, y0):
+                return vbuf[l, own + xq + i, pl.ds(y0, 8)]
+
+            def put(i, y0, v):
+                vbuf[nxt, own + xq + i, pl.ds(y0, 8)] = v
+
+            y_compute(window_of, old, put, ty, tz, w4, bias[pl.ds(l, 1), :])
 
     def zero_planes(l):
         vbuf[l, pl.ds(own + x_of(NCH - 1), CH)] = jnp.zeros((CH, BY, ZL, LANES), BF16)
@@ -236,11 +264,11 @@
     x_seg(0, 0, 0)
     with jax.named_scope("barrier"):
         pl.semaphore_wait(barrier, neighbours)
-    y_send(0, 0, 0)
+    y_send(0, 0, 1)
     load(1).wait()
     pack(1, x_head, HEAD, *SEGS[1])
     x_seg(0, 0, 1)
-    y_send(0, 0, 1)
+    y_send(0, 0, 0)
     load(2).wait()
     pack(2, x_rest, BX - HEAD, 0, BY)
     x_copy(0).start()
@@ -274,14 +302,25 @@
         def _():
             zero_halo(l, H + BY)
 
+        @pl.when(l == LAYERS - 1)
+        def _():
+            store(NQ - 1).start()
+            for mat in store_mats:
+                mat.start()
+            store_u.start()
+            for edge, copy in store_edges:
+                pl.when(edge)(copy.start)
+
         def ys(q, c):
             @pl.when((q == NQ - CH // QUAD) & (l < LAYERS - 1))
             def _():
                 x_pass(l + 1, 0)
 
-            y_quad(l, q)
-
-            @pl.when(l == LAYERS - 1)
+            @pl.when((q < NQ - 1) | (l < LAYERS - 1))
+            def _():
+                y_quad(l, q)
+
+            @pl.when((q < NQ - 1) & (l == LAYERS - 1))
             def _():
                 store(q).start()
 
@@ -299,7 +338,15 @@
         xs = xq_of(q)
         return pltpu.make_async_copy(vbuf.at[LAYERS - 1, pl.ds(own + xs, QUAD)], out.at[pl.ds(xs, QUAD)], out_sem)
 
+    store_mats = [pltpu.make_async_copy(m, o, small_sem.at[n]) for n, (m, o) in enumerate(((ty, ty_out), (tz, tz_out), (w4, w4_out)))]
+    last_u = ubuf.at[LAYERS - 1, pl.ds(xq_of(NQ - 1), QUAD)]
+    store_u = pltpu.make_async_copy(last_u.at[:, pl.ds(H, BY)], u_out.at[:, pl.ds(H, BY)], in_sem.at[0])
+    store_edges = [
+        (jnp.logical_not(has), pltpu.make_async_copy(last_u.at[:, pl.ds(y0, H)], u_out.at[:, pl.ds(y0, H)], in_sem.at[n]))
+        for has, y0, n in ((has_left, 0, 2), (has_right, H + BY, 3))
+    ]
     lax.fori_loop(0, LAYERS, layer, 0)
+    y_wait(LAYERS - 1, NQ - 1)
 
     with jax.named_scope("finish"):
         for side in range(2):
@@ -312,31 +359,66 @@
                     device_id={COL_AXIS: left if side == 0 else right}).wait_send()
 
         pltpu.make_async_copy(vbuf.at[LAYERS - 1, pl.ds(own, BX)], out, out_sem).wait()
-
-
-def unpack_kernel(src, dst, got, buf, in_sems, out_sem):
-    def read(p):
-        xs = pl.ds(p * PART, PART)
-        return pltpu.make_async_copy(src.at[xs], got.at[xs], in_sems.at[p])
-
-    def write(p):
-        xs = pl.ds(p * PART, PART)
-        return pltpu.make_async_copy(buf.at[xs], dst.at[xs], out_sem)
-
-    for p in range(BX // PART):
-        read(p).start()
-
-    def body(p, carry):
-        xs = pl.ds(p * PART, PART)
-        read(p).wait()
-        s = got[xs]
-        buf[xs, :, :ZL, :] = s[:, :, :, :C]
-        buf[xs, :, ZL:, :] = s[:, :, :, C:]
-        write(p).start()
+        for edge, copy in store_edges:
+            pl.when(edge)(copy.wait)
+        for mat in store_mats:
+            mat.wait()
+        store_u.wait()
+
+
+def unpack(s):
+    r = pltpu.roll(s.reshape(QUAD * BY * ZL, LANES), C, 1).reshape(QUAD, BY, ZL, LANES)
+    return s[:, :, :, :C], r[:, :, :, :C]
+
+
+def last_kernel(src, u_hbm, ty_hbm, tz_hbm, w4_hbm, bias_hbm, dst, got, u, ty, tz, w4, bias, buf, in_sems, mat_sems, out_sem):
+    xi = lax.axis_index(ROW_AXIS)
+
+    def planes(q):
+        return pl.ds(jnp.where(xi == 0, QUAD * q, BX - QUAD - QUAD * q), QUAD)
+
+    def read(q):
+        return pltpu.make_async_copy(src.at[planes(q)], got.at[planes(q)], in_sems.at[q])
+
+    def write(q):
+        return pltpu.make_async_copy(buf.at[planes(q)], dst.at[planes(q)], out_sem)
+
+    mats = [
+        pltpu.make_async_copy(h, v, mat_sems.at[n])
+        for n, (h, v) in enumerate(((u_hbm, u), (ty_hbm, ty), (tz_hbm, tz), (w4_hbm, w4), (bias_hbm, bias)))
+    ]
+    for q in range(NQ - 1):
+        read(q).start()
+    for mat in mats:
+        mat.start()
+    read(NQ - 1).start()
+
+    def body(q, carry):
+        read(q).wait()
+        buf[planes(q), :, :ZL, :], buf[planes(q), :, ZL:, :] = unpack(got[planes(q)])
+        write(q).start()
         return carry
 
-    lax.fori_loop(0, BX // PART, body, 0)
-    pltpu.make_async_copy(buf, dst, out_sem).wait()
+    with jax.named_scope("unpack"):
+        lax.fori_loop(0, NQ - 1, body, 0)
+    with jax.named_scope("matwait"):
+        for mat in mats:
+            mat.wait()
+        read(NQ - 1).wait()
+    xq = jnp.where(xi == 0, BX - QUAD, 0)
+
+    def put(i, y0, v):
+        buf[xq + i, pl.ds(y0, 8), :ZL, :] = v[:, :, :C]
+        buf[xq + i, pl.ds(y0, 8), ZL:, :] = v[:, :, C:]
+
+    with jax.named_scope("ycomp"):
+        y_compute(
+            lambda i, y0: u[i, pl.ds(y0, WIN)], lambda i, y0: got[xq + i, pl.ds(y0, 8)], put,
+            ty, tz, w4, bias[pl.ds(LAYERS - 1, 1), :])
+    write(NQ - 1).start()
+
+    with jax.named_scope("outwait"):
+        pltpu.make_async_copy(buf, dst, out_sem).wait()
 
 
 def solution(mesh):
@@ -346,11 +428,13 @@
 
     def local_layers(volume, filter_taps, mix_weights, mix_bias):
         vol = jnp.transpose(volume, (1, 2, 3, 0))
-        packed = pl.pallas_call(
+        toeplitz = (CH * ZL, WIN * ZL)
+        passed_shapes = ((BX, BY, ZL, LANES), (QUAD, YS, ZL, LANES), toeplitz, (8 * BZ, 8 * BZ), (4 * C, 4 * C))
+        passed = pl.pallas_call(
             functools.partial(kernel, y_count),
-            out_shape=jax.ShapeDtypeStruct((BX, BY, ZL, LANES), BF16),
+            out_shape=[jax.ShapeDtypeStruct(shape, BF16) for shape in passed_shapes],
             in_specs=[any_spec] * 4,
-            out_specs=any_spec,
+            out_specs=[any_spec] * 5,
             scratch_shapes=[
                 pltpu.VMEM((BX, BY, BZ, C), BF16),
                 pltpu.VMEM((LAYERS, XS, BY, ZL, LANES), BF16),
@@ -373,18 +457,19 @@
             compiler_params=pltpu.CompilerParams(collective_id=0, has_side_effects=True, vmem_limit_bytes=60 * 2**20),
         )(vol, filter_taps, mix_weights, mix_bias)
         result = pl.pallas_call(
-            unpack_kernel,
+            last_kernel,
             out_shape=jax.ShapeDtypeStruct((BX, BY, BZ, C), BF16),
-            in_specs=[any_spec],
+            in_specs=[any_spec] * 6,
             out_specs=any_spec,
-            scratch_shapes=[
-                pltpu.VMEM((BX, BY, ZL, LANES), BF16),
+            scratch_shapes=[pltpu.VMEM(shape, BF16) for shape in passed_shapes] + [
+                pltpu.VMEM((LAYERS, C), F32),
                 pltpu.VMEM((BX, BY, BZ, C), BF16),
-                pltpu.SemaphoreType.DMA((BX // PART,)),
+                pltpu.SemaphoreType.DMA((NQ,)),
+                pltpu.SemaphoreType.DMA((5,)),
                 pltpu.SemaphoreType.DMA,
             ],
             compiler_params=pltpu.CompilerParams(vmem_limit_bytes=60 * 2**20),
-        )(packed)
+        )(*passed, mix_bias)
         return jnp.transpose(result, (3, 0, 1, 2))
 
     return jax.shard_map(local_layers, mesh=mesh, in_specs=(vol_spec, P(), P(), P()), out_specs=vol_spec, check_vma=False)

time: 100 us -> 99 us (0.990)
  Pallas kernels: 100 us -> 98.9 us
    pallas_call x2, Pallas kernels: 100 us -> 98.9 us  [the longest x1 93.5 us: local_layers(): pl.pallas_call(functools.partial(kernel, y_count), out_shape=[jax.ShapeDt...]
where the time goes in v5:
time: 99 us; the launch traced here: 98.9 us
  Pallas kernels  98.9 us (100%)
    pallas_call x1, Pallas kernels, local_layers(): pl.pallas_call(functools.partial(kernel, y_count), out_shape=[jax.ShapeDt...  93.5 us
    pallas_call x1, Pallas kernels, local_layers(): pl.pallas_call(last_kernel, out_shape=jax.ShapeDtypeStruct((BX, BY, BZ, C...  5.43 us

profile of v5, /device:TPU:96, one launch (start us, length us, event | category | flops | bytes accessed | tf_op | source)
XLA Modules:
  0.0 98.9 jit_solution(16479689826061100246)
XLA Ops:
  0.0 93.5 %shard_map.46 = (bf16[32,32,16,128]{3,2,1,0:T(8,128)(2,1)}, bf16[4,52,16,128]{3,2,1,0:T(8,128)(2,1)}, bf16[128,448]{1,0:T(8,128)(2,1)}, bf16[256,256]{1,0:T(8,128)(2,1)}, bf16[256,256]{1,0:T(8,128)(2,1)}) custom-call(bf16[32,32,32,64]{3,2,1,0:T(8,128)(2,1)} %bitcast.2, f32[3,3,21]{2,1,0:T(4,128)} %taps_hbm.1, bf16[3,64,64]{2,1,0:T(8,128)(2,1)} %wmat_hbm.1, ...), custom_call_target="tpu_custom_call" | custom-call | tf_op jit(solution)/shard_map/pallas_call | solution.py:433
  93.5 5.4 %shard_map.47 = bf16[32,32,32,64]{3,2,1,0:T(8,128)(2,1)} custom-call(bf16[32,32,16,128]{3,2,1,0:T(8,128)(2,1)} %get-tuple-element.10.src, bf16[4,52,16,128]{3,2,1,0:T(8,128)(2,1)} %get-tuple-element.11.u_hbm, bf16[128,448]{1,0:T(8,128)(2,1)} %get-tuple-element.12.ty_hbm, bf16[256,256]{1,0:T(8,128)(2,1)} %get-tuple-element.13.tz_hbm, ...), custom_call_target="tpu_custom_call" | custom-call | tf_op jit(solution)/shard_map/pallas_call | solution.py:459

commit v6 on v5

--- a/solution.py
+++ b/solution.py
@@ -24,7 +24,8 @@
 QUAD = 4
 NQ = BX // QUAD
 WIN = CH + 2 * H
-HEAD = CH + H
+EARLY = -(-(CH + H) // QUAD)
+HEAD = QUAD + H
 XS = BX + H
 YS = BY + 2 * H
 SEGS = ((BY - H, H), (0, H), (H, BY - 2 * H))
@@ -72,7 +73,7 @@
             put(i, 8 * g, (old(i, 8 * g).astype(F32) + mi).astype(BF16))
 
 
-def kernel(y_count, vol, taps_hbm, wmat_hbm, bias_hbm, out, u_out, ty_out, tz_out, w4_out, stage, vbuf, ubuf, tx, ty, tz, w4, taps, wmat, bias, in_sem, small_sem, out_sem, ysend, yrecv, xsend, xrecv):
+def kernel(y_count, vol, taps_hbm, wmat_hbm, bias_hbm, out, u_out, ty_out, tz_out, w4_out, stage, vbuf, ubuf, tq, tx, ty, tz, w4, taps, wmat, bias, in_sem, small_sem, out_sem, ysend, yrecv, xsend, xrecv):
     xi = lax.axis_index(ROW_AXIS)
     yi = lax.axis_index(COL_AXIS)
     own = xi * H
@@ -80,6 +81,19 @@
     has_right = yi < y_count - 1
     left = lax.rem(yi + y_count - 1, y_count)
     right = lax.rem(yi + 1, y_count)
+
+    barrier = pltpu.get_barrier_semaphore()
+
+    @pl.when(has_left)
+    def _():
+        pl.semaphore_signal(barrier, inc=1, device_id={COL_AXIS: left})
+
+    @pl.when(has_right)
+    def _():
+        pl.semaphore_signal(barrier, inc=1, device_id={COL_AXIS: right})
+
+    pl.semaphore_signal(barrier, inc=1, device_id={ROW_AXIS: 1 - xi})
+    neighbours = 1 + has_left.astype(jnp.int32) + has_right.astype(jnp.int32)
 
     def x_of(k):
         return jnp.where(xi == 0, CH * k, BX - CH - CH * k)
@@ -106,19 +120,6 @@
     small[1].start()
     small[2].start()
 
-    barrier = pltpu.get_barrier_semaphore()
-
-    @pl.when(has_left)
-    def _():
-        pl.semaphore_signal(barrier, inc=1, device_id={COL_AXIS: left})
-
-    @pl.when(has_right)
-    def _():
-        pl.semaphore_signal(barrier, inc=1, device_id={COL_AXIS: right})
-
-    pl.semaphore_signal(barrier, inc=1, device_id={ROW_AXIS: 1 - xi})
-    neighbours = 1 + has_left.astype(jnp.int32) + has_right.astype(jnp.int32)
-
     def y_copy(l, q, side):
         xs = pl.ds(xq_of(q), QUAD)
         src = ubuf.at[l, xs, pl.ds(H, H)] if side == 0 else ubuf.at[l, xs, pl.ds(BY, H)]
@@ -143,15 +144,17 @@
             w0, slot = window(k)
             tx[...] = band_times_eye(lambda n: taps[l, 0, n], CH * ZL, WIN * ZL, ZL, w0 - slot + H)
 
+    def x_rows(l, mat, w0, width, x0, count, seg):
+        with jax.named_scope("xseg"):
+            first, ny = SEGS[seg]
+            cols = [vbuf[l, pl.ds(w0, width), first + i].reshape(width * ZL, LANES) for i in range(ny)]
+            r = jnp.dot(mat, jnp.concatenate(cols, axis=1), preferred_element_type=F32).astype(BF16)
+            for i in range(ny):
+                ubuf[l, pl.ds(x0, count), H + first + i] = r[:, LANES * i:LANES * (i + 1)].reshape(count, ZL, LANES)
+
     def x_seg(l, k, seg):
-        with jax.named_scope("xseg"):
-            w0, _ = window(k)
-            x0 = x_of(k)
-            first, count = SEGS[seg]
-            cols = [vbuf[l, pl.ds(w0, WIN), first + i].reshape(WIN * ZL, LANES) for i in range(count)]
-            r = jnp.dot(tx[...], jnp.concatenate(cols, axis=1), preferred_element_type=F32).astype(BF16)
-            for i in range(count):
-                ubuf[l, pl.ds(x0, CH), H + first + i] = r[:, LANES * i:LANES * (i + 1)].reshape(CH, ZL, LANES)
+        w0, _ = window(k)
+        x_rows(l, tx[...], w0, WIN, x_of(k), CH, seg)
 
     def last_copy(side):
         l, q = LAYERS - 1, NQ - 1
@@ -160,19 +163,21 @@
             src_ref=src, dst_ref=u_out.at[:, pl.ds(H + BY if side == 0 else 0, H)], send_sem=ysend.at[side], recv_sem=yrecv.at[l, q],
             device_id={COL_AXIS: left if side == 0 else right})
 
+    def send_quad(l, q, side):
+        goes = has_left if side == 0 else has_right
+        last = (l == LAYERS - 1) & (q == NQ - 1)
+
+        @pl.when(goes & jnp.logical_not(last))
+        def _():
+            y_copy(l, q, side).start()
+
+        @pl.when(goes & last)
+        def _():
+            last_copy(side).start()
+
     def y_send(l, k, side):
-        goes = has_left if side == 0 else has_right
         for j in range(CH // QUAD):
-            q = k * (CH // QUAD) + j
-            last = (l == LAYERS - 1) & (q == NQ - 1)
-
-            @pl.when(goes & jnp.logical_not(last))
-            def _():
-                y_copy(l, q, side).start()
-
-            @pl.when(goes & last)
-            def _():
-                last_copy(side).start()
+            send_quad(l, k * (CH // QUAD) + j, side)
 
     def x_pass(l, k):
         x_mat(l, k)
@@ -232,7 +237,7 @@
             y_compute(window_of, old, put, ty, tz, w4, bias[pl.ds(l, 1), :])
 
     def zero_planes(l):
-        vbuf[l, pl.ds(own + x_of(NCH - 1), CH)] = jnp.zeros((CH, BY, ZL, LANES), BF16)
+        vbuf[l, pl.ds(own + jnp.where(xi == 0, QUAD * EARLY, 0), BX - QUAD * EARLY)] = jnp.zeros((BX - QUAD * EARLY, BY, ZL, LANES), BF16)
 
     def zero_halo(l, y0):
         def body(n, carry):
@@ -252,29 +257,30 @@
 
             lax.fori_loop(0, count, body, 0, unroll=True)
 
-    with jax.named_scope("zero0"):
-        for seg in range(2):
-            first, ny = SEGS[seg]
-            pad = WIN - HEAD
-            vbuf[0, pl.ds(own + jnp.where(xi == 0, HEAD, BX - WIN), pad), pl.ds(first, ny)] = jnp.zeros((pad, ny, ZL, LANES), BF16)
     small[0].wait()
+    slot = own + xq_of(0)
+    w0 = own + x_head
+    tq[...] = band_times_eye(lambda n: taps[0, 0, n], QUAD * ZL, HEAD * ZL, ZL, w0 - slot + H)
+    for seg in range(2):
+        load(seg).wait()
+        pack(seg, x_head, HEAD, *SEGS[seg])
+        x_rows(0, tq[...], w0, HEAD, xq_of(0), QUAD, seg)
+        if seg == 0:
+            with jax.named_scope("barrier"):
+                pl.semaphore_wait(barrier, neighbours)
+        send_quad(0, 0, 1 - seg)
     x_mat(0, 0)
-    load(0).wait()
-    pack(0, x_head, HEAD, *SEGS[0])
-    x_seg(0, 0, 0)
-    with jax.named_scope("barrier"):
-        pl.semaphore_wait(barrier, neighbours)
-    y_send(0, 0, 1)
-    load(1).wait()
-    pack(1, x_head, HEAD, *SEGS[1])
-    x_seg(0, 0, 1)
-    y_send(0, 0, 0)
     load(2).wait()
     pack(2, x_rest, BX - HEAD, 0, BY)
     x_copy(0).start()
+    second = tx[pl.ds(jnp.where(xi == 0, QUAD * ZL, 0), QUAD * ZL), :]
+    for seg in range(2):
+        x_rows(0, second, window(0)[0], WIN, xq_of(1), QUAD, seg)
+        send_quad(0, 1, 1 - seg)
     load(3).wait()
     pack(3, x_head, HEAD, *SEGS[2])
     x_seg(0, 0, 2)
+    x_pass(0, 1)
     for l in range(1, LAYERS):
         zero_planes(l)
     small[1].wait()
@@ -290,7 +296,7 @@
             x_pass(l, k)
             return c
 
-        lax.fori_loop(1, NCH, xs, 0)
+        lax.fori_loop(2, NCH, xs, 0)
         with jax.named_scope("mats"):
             layer_mats(l)
 
@@ -312,9 +318,9 @@
                 pl.when(edge)(copy.start)
 
         def ys(q, c):
-            @pl.when((q == NQ - CH // QUAD) & (l < LAYERS - 1))
-            def _():
-                x_pass(l + 1, 0)
+            @pl.when(((q == EARLY) | (q == NQ - 1)) & (l < LAYERS - 1))
+            def _():
+                x_pass(l + 1, jnp.where(q == EARLY, 0, 1))
 
             @pl.when((q < NQ - 1) | (l < LAYERS - 1))
             def _():
@@ -439,8 +445,9 @@
                 pltpu.VMEM((BX, BY, BZ, C), BF16),
                 pltpu.VMEM((LAYERS, XS, BY, ZL, LANES), BF16),
                 pltpu.VMEM((LAYERS, BX, YS, ZL, LANES), BF16),
-                pltpu.VMEM((CH * ZL, WIN * ZL), BF16),
-                pltpu.VMEM((CH * ZL, WIN * ZL), BF16),
+                pltpu.VMEM((QUAD * ZL, HEAD * ZL), BF16),
+                pltpu.VMEM(toeplitz, BF16),
+                pltpu.VMEM(toeplitz, BF16),
                 pltpu.VMEM((8 * BZ, 8 * BZ), BF16),
                 pltpu.VMEM((4 * C, 4 * C), BF16),
                 pltpu.SMEM((LAYERS, 3, TAPS), F32),

time: 99 us -> 98 us (0.990)
  Pallas kernels: 98.9 us -> 97.9 us
    pallas_call x1, Pallas kernels: 93.5 us -> 92.5 us  [local_layers(): pl.pallas_call(functools.partial(kernel, y_count), out_shape=[jax.ShapeDt...]
where the time goes in v6:
time: 98 us; the launch traced here: 97.9 us
  Pallas kernels  97.9 us (100%)
    pallas_call x1, Pallas kernels, local_layers(): pl.pallas_call(functools.partial(kernel, y_count), out_shape=[jax.ShapeDt...  92.5 us
    pallas_call x1, Pallas kernels, local_layers(): pl.pallas_call(last_kernel, out_shape=jax.ShapeDtypeStruct((BX, BY, BZ, C...  5.43 us

profile of v6, /device:TPU:96, one launch (start us, length us, event | category | flops | bytes accessed | tf_op | source)
XLA Modules:
  0.0 97.9 jit_solution(3686399237674232461)
XLA Ops:
  0.0 92.5 %shard_map.46 = (bf16[32,32,16,128]{3,2,1,0:T(8,128)(2,1)}, bf16[4,52,16,128]{3,2,1,0:T(8,128)(2,1)}, bf16[128,448]{1,0:T(8,128)(2,1)}, bf16[256,256]{1,0:T(8,128)(2,1)}, bf16[256,256]{1,0:T(8,128)(2,1)}) custom-call(bf16[32,32,32,64]{3,2,1,0:T(8,128)(2,1)} %bitcast.2, f32[3,3,21]{2,1,0:T(4,128)} %taps_hbm.1, bf16[3,64,64]{2,1,0:T(8,128)(2,1)} %wmat_hbm.1, ...), custom_call_target="tpu_custom_call" | custom-call | tf_op jit(solution)/shard_map/pallas_call | solution.py:439
  92.5 5.4 %shard_map.47 = bf16[32,32,32,64]{3,2,1,0:T(8,128)(2,1)} custom-call(bf16[32,32,16,128]{3,2,1,0:T(8,128)(2,1)} %get-tuple-element.10.src, bf16[4,52,16,128]{3,2,1,0:T(8,128)(2,1)} %get-tuple-element.11.u_hbm, bf16[128,448]{1,0:T(8,128)(2,1)} %get-tuple-element.12.ty_hbm, bf16[256,256]{1,0:T(8,128)(2,1)} %get-tuple-element.13.tz_hbm, ...), custom_call_target="tpu_custom_call" | custom-call | tf_op jit(solution)/shard_map/pallas_call | solution.py:466

commit v7 on v6

--- a/solution.py
+++ b/solution.py
@@ -24,6 +24,7 @@
 QUAD = 4
 NQ = BX // QUAD
 WIN = CH + 2 * H
+BEFORE = 5
 EARLY = -(-(CH + H) // QUAD)
 HEAD = QUAD + H
 XS = BX + H
@@ -43,13 +44,14 @@
     return jnp.where(i % inner == j % inner, acc, 0.0).astype(BF16)
 
 
-def y_compute(window_of, old, put, ty, tz, w4, b):
+def y_compute(window_of, old, put, ty, tz, w4, b, between=lambda stage: None):
     b = jnp.concatenate([b, b], axis=1)
     b = jnp.concatenate([b, b], axis=1)
     rs, ss = [], []
     for g in range(BY // 8):
         cols = [window_of(i, 8 * g).reshape(WIN * ZL, LANES) for i in range(QUAD)]
         rs.append(jnp.dot(ty[...], jnp.concatenate(cols, axis=1), preferred_element_type=F32).astype(BF16))
+    between(0)
     for g in range(BY // 8):
         zs = []
         for i in range(QUAD):
@@ -60,6 +62,7 @@
             zs.append(jnp.concatenate([lo, hi], axis=1).reshape(4 * BZ, LANES))
         dz = jnp.concatenate([jnp.concatenate(zs[:2], axis=0), jnp.concatenate(zs[2:], axis=0)], axis=1)
         ss.append(jnp.dot(tz[...], dz, preferred_element_type=F32).astype(BF16))
+    between(1)
     for g in range(BY // 8):
         lhs = []
         for h in range(2):
@@ -399,14 +402,26 @@
         mat.start()
     read(NQ - 1).start()
 
+    def turn(q):
+        buf[planes(q), :, :ZL, :], buf[planes(q), :, ZL:, :] = unpack(got[planes(q)])
+
     def body(q, carry):
         read(q).wait()
-        buf[planes(q), :, :ZL, :], buf[planes(q), :, ZL:, :] = unpack(got[planes(q)])
+        turn(q)
         write(q).start()
         return carry
 
+    def between(stage):
+        for q in range(BEFORE, NQ - 1):
+            if stage == 0:
+                turn(q)
+            else:
+                write(q).start()
+
     with jax.named_scope("unpack"):
-        lax.fori_loop(0, NQ - 1, body, 0)
+        lax.fori_loop(0, BEFORE, body, 0)
+        for q in range(BEFORE, NQ - 1):
+            read(q).wait()
     with jax.named_scope("matwait"):
         for mat in mats:
             mat.wait()
@@ -420,7 +435,7 @@
     with jax.named_scope("ycomp"):
         y_compute(
             lambda i, y0: u[i, pl.ds(y0, WIN)], lambda i, y0: got[xq + i, pl.ds(y0, 8)], put,
-            ty, tz, w4, bias[pl.ds(LAYERS - 1, 1), :])
+            ty, tz, w4, bias[pl.ds(LAYERS - 1, 1), :], between)
     write(NQ - 1).start()
 
     with jax.named_scope("outwait"):

time: 98 us -> 97.7 us (level)
  no operation moved by 1% of the time
where the time goes in v7:
time: 97.7 us; the launch traced here: 97.6 us
  Pallas kernels  97.5 us (100%)
    pallas_call x1, Pallas kernels, local_layers(): pl.pallas_call(functools.partial(kernel, y_count), out_shape=[jax.ShapeDt...  92.5 us
    pallas_call x1, Pallas kernels, local_layers(): pl.pallas_call(last_kernel, out_shape=jax.ShapeDtypeStruct((BX, BY, BZ, C...  5.07 us

profile of v7, /device:TPU:96, one launch (start us, length us, event | category | flops | bytes accessed | tf_op | source)
XLA Modules:
  0.0 97.6 jit_solution(7259774573847312347)
XLA Ops:
  0.0 92.5 %shard_map.46 = (bf16[32,32,16,128]{3,2,1,0:T(8,128)(2,1)}, bf16[4,52,16,128]{3,2,1,0:T(8,128)(2,1)}, bf16[128,448]{1,0:T(8,128)(2,1)}, bf16[256,256]{1,0:T(8,128)(2,1)}, bf16[256,256]{1,0:T(8,128)(2,1)}) custom-call(bf16[32,32,32,64]{3,2,1,0:T(8,128)(2,1)} %bitcast.2, f32[3,3,21]{2,1,0:T(4,128)} %taps_hbm.1, bf16[3,64,64]{2,1,0:T(8,128)(2,1)} %wmat_hbm.1, ...), custom_call_target="tpu_custom_call" | custom-call | tf_op jit(solution)/shard_map/pallas_call | solution.py:454
  92.5 5.1 %shard_map.47 = bf16[32,32,32,64]{3,2,1,0:T(8,128)(2,1)} custom-call(bf16[32,32,16,128]{3,2,1,0:T(8,128)(2,1)} %get-tuple-element.10.src, bf16[4,52,16,128]{3,2,1,0:T(8,128)(2,1)} %get-tuple-element.11.u_hbm, bf16[128,448]{1,0:T(8,128)(2,1)} %get-tuple-element.12.ty_hbm, bf16[256,256]{1,0:T(8,128)(2,1)} %get-tuple-element.13.tz_hbm, ...), custom_call_target="tpu_custom_call" | custom-call | tf_op jit(solution)/shard_map/pallas_call | solution.py:481

commit v8 on v7

--- a/solution.py
+++ b/solution.py
@@ -128,7 +128,7 @@
         src = ubuf.at[l, xs, pl.ds(H, H)] if side == 0 else ubuf.at[l, xs, pl.ds(BY, H)]
         dst = ubuf.at[l, xs, pl.ds(H + BY, H)] if side == 0 else ubuf.at[l, xs, pl.ds(0, H)]
         return pltpu.make_async_remote_copy(
-            src_ref=src, dst_ref=dst, send_sem=ysend.at[side], recv_sem=yrecv.at[l, q],
+            src_ref=src, dst_ref=dst, send_sem=ysend.at[side], recv_sem=yrecv.at[l % 2, q],
             device_id={COL_AXIS: left if side == 0 else right})
 
     def x_copy(l):
@@ -136,7 +136,7 @@
         dst = jnp.where(xi == 0, 0, BX)
         return pltpu.make_async_remote_copy(
             src_ref=vbuf.at[l, pl.ds(src, H)], dst_ref=vbuf.at[l, pl.ds(dst, H)],
-            send_sem=xsend.at[l], recv_sem=xrecv.at[l], device_id={ROW_AXIS: 1 - xi})
+            send_sem=xsend, recv_sem=xrecv.at[l % 2], device_id={ROW_AXIS: 1 - xi})
 
     def window(k):
         slot = own + x_of(k)
@@ -163,7 +163,7 @@
         l, q = LAYERS - 1, NQ - 1
         src = ubuf.at[l, pl.ds(xq_of(q), QUAD), pl.ds(H if side == 0 else BY, H)]
         return pltpu.make_async_remote_copy(
-            src_ref=src, dst_ref=u_out.at[:, pl.ds(H + BY if side == 0 else 0, H)], send_sem=ysend.at[side], recv_sem=yrecv.at[l, q],
+            src_ref=src, dst_ref=u_out.at[:, pl.ds(H + BY if side == 0 else 0, H)], send_sem=ysend.at[side], recv_sem=yrecv.at[l % 2, q],
             device_id={COL_AXIS: left if side == 0 else right})
 
     def send_quad(l, q, side):
@@ -215,7 +215,7 @@
             @pl.when(has_left & has_right)
             def _():
                 pltpu.make_async_remote_copy(
-                    src_ref=both, dst_ref=both, send_sem=ysend.at[0], recv_sem=yrecv.at[l, q],
+                    src_ref=both, dst_ref=both, send_sem=ysend.at[0], recv_sem=yrecv.at[l % 2, q],
                     device_id={COL_AXIS: left}).wait_recv()
 
             @pl.when(jnp.logical_not(has_left & has_right))
@@ -472,9 +472,9 @@
                 pltpu.SemaphoreType.DMA((3,)),
                 pltpu.SemaphoreType.DMA,
                 pltpu.SemaphoreType.DMA((2,)),
-                pltpu.SemaphoreType.DMA((LAYERS, NQ)),
-                pltpu.SemaphoreType.DMA((LAYERS,)),
-                pltpu.SemaphoreType.DMA((LAYERS,)),
+                pltpu.SemaphoreType.DMA((2, NQ)),
+                pltpu.SemaphoreType.DMA,
+                pltpu.SemaphoreType.DMA((2,)),
             ],
             compiler_params=pltpu.CompilerParams(collective_id=0, has_side_effects=True, vmem_limit_bytes=60 * 2**20),
         )(vol, filter_taps, mix_weights, mix_bias)

time: 97.7 us -> 97.6 us (level)
  no operation moved by 1% of the time
where the time goes in v8:
time: 97.6 us; the launch traced here: 97.5 us
  Pallas kernels  97.4 us (100%)
    pallas_call x1, Pallas kernels, local_layers(): pl.pallas_call(functools.partial(kernel, y_count), out_shape=[jax.ShapeDt...  92.4 us
    pallas_call x1, Pallas kernels, local_layers(): pl.pallas_call(last_kernel, out_shape=jax.ShapeDtypeStruct((BX, BY, BZ, C...  5.07 us

profile of v8, /device:TPU:96, one launch (start us, length us, event | category | flops | bytes accessed | tf_op | source)
XLA Modules:
  0.0 97.5 jit_solution(9824628736543195746)
XLA Ops:
  0.0 92.4 %shard_map.46 = (bf16[32,32,16,128]{3,2,1,0:T(8,128)(2,1)}, bf16[4,52,16,128]{3,2,1,0:T(8,128)(2,1)}, bf16[128,448]{1,0:T(8,128)(2,1)}, bf16[256,256]{1,0:T(8,128)(2,1)}, bf16[256,256]{1,0:T(8,128)(2,1)}) custom-call(bf16[32,32,32,64]{3,2,1,0:T(8,128)(2,1)} %bitcast.2, f32[3,3,21]{2,1,0:T(4,128)} %taps_hbm.1, bf16[3,64,64]{2,1,0:T(8,128)(2,1)} %wmat_hbm.1, ...), custom_call_target="tpu_custom_call" | custom-call | tf_op jit(solution)/shard_map/pallas_call | solution.py:454
  92.4 5.1 %shard_map.47 = bf16[32,32,32,64]{3,2,1,0:T(8,128)(2,1)} custom-call(bf16[32,32,16,128]{3,2,1,0:T(8,128)(2,1)} %get-tuple-element.10.src, bf16[4,52,16,128]{3,2,1,0:T(8,128)(2,1)} %get-tuple-element.11.u_hbm, bf16[128,448]{1,0:T(8,128)(2,1)} %get-tuple-element.12.ty_hbm, bf16[256,256]{1,0:T(8,128)(2,1)} %get-tuple-element.13.tz_hbm, ...), custom_call_target="tpu_custom_call" | custom-call | tf_op jit(solution)/shard_map/pallas_call | solution.py:481
